TPU v7x, 32 devices: a whole 2x2x4 slice. The times are simulated.
32 devices in a mesh: gx: 4 (over y, x), gy: 4 (over z), gz: 2 (over core).
Axes of the slice: x: 2, y: 2, z: 4, core: 2. Of those that a mesh axis runs over, the one named last changes fastest.
Arguments:
- start: float32 [4, 4, 2, 1, 32, 1024], P('gx', 'gy', 'gz'), may hold values from -6 to 6
- stencils: float32 [6, 4, 4, 2, 32, 32], P(None, 'gx', 'gy', 'gz'), as said below
Outputs:
- basis: float32 [4, 4, 2, 1, 5, 32, 1024], P('gx', 'gy', 'gz')
- coefficients: float32 [1, 2, 5], replicated
Inputs may be any that keep to these rules, and one draw needn't show every extreme that they name: `stencils`: each of a patch's six matrices is symmetric positive definite.
All inputs are finite; a program needn't handle non-finite values.
Results may differ from a plain program's by a relative error of at most 0.0003.
Values sent between devices are 32-bit elements; how exact they have to be, the bound alone decides.
A program may use at most 128 MiB of HBM per device.

v0:
```python
import functools

import jax
import jax.numpy as jnp
from jax import lax
from jax.experimental import pallas as pl
from jax.experimental.pallas import tpu as pltpu
from jax.sharding import PartitionSpec as P

ITERS = 5
LANES = 128
SUB = 8
MESH = pl.DeviceIdType.MESH
F32 = jnp.float32
BF16 = jnp.bfloat16
HIGHEST = lax.Precision.HIGHEST


def iota(shape, dim):
    return lax.broadcasted_iota(jnp.int32, shape, dim)


def split(x):
    hi = x.astype(BF16)
    return hi, (x - hi.astype(F32)).astype(BF16)


def exact(a, b):
    return lax.dot_general(a, b, (((1,), (0,)), ((), ())), precision=HIGHEST, preferred_element_type=F32)


def mul(a, b):
    return jnp.dot(a, b, preferred_element_type=F32)


def swap(x):
    sub = iota((1, SUB, LANES), 1)
    group = iota((1, SUB, LANES), 2) >> 5
    s0, s1 = sub & 1, (sub >> 1) & 1
    g0, g1 = group & 1, (group >> 1) & 1
    far = pltpu.roll(x, 64, 2)
    x = jnp.where(s1 == g1, x, jnp.where(s1 == 0, pltpu.roll(far, SUB - 2, 1), pltpu.roll(far, 2, 1)))
    up = pltpu.roll(pltpu.roll(x, SUB - 1, 1), 32, 2)
    down = pltpu.roll(pltpu.roll(x, 1, 1), LANES - 32, 2)
    return jnp.where(s0 == g0, x, jnp.where(s0 == 0, up, down))


def build_matrices(st, mx, my, mz):
    count = st.shape[1]
    wide = LANES
    spread = ((iota((wide, count), 0) & (count - 1)) == iota((wide, count), 1)).astype(F32)
    spread_t = ((iota((count, wide), 1) & (count - 1)) == iota((count, wide), 0)).astype(F32)
    same = (iota((wide, wide), 0) >> 5) == (iota((wide, wide), 1) >> 5)
    for slot, which in ((0, 5), (1, 2)):
        big = exact(exact(spread, st[which].T), spread_t)
        hi, lo = split(jnp.where(same, big, 0.0))
        mz[0:wide, slot * wide:(slot + 1) * wide] = hi
        mz[wide:2 * wide, slot * wide:(slot + 1) * wide] = hi
        mz[2 * wide:3 * wide, slot * wide:(slot + 1) * wide] = lo
    rows = 2 * count
    r = iota((rows, count), 0)
    pick = (((r >> 3) * 4 + (r & 3)) == iota((rows, count), 1)).astype(F32)
    cols = 3 * rows
    l = iota((count, cols), 1) & (rows - 1)
    pick_t = (((l >> 3) * 4 + (l & 3)) == iota((count, cols), 0)).astype(F32)
    same = ((iota((rows, cols), 0) >> 2) & 1) == ((iota((rows, cols), 1) >> 2) & 1)
    middle = (iota((rows, cols), 1) >= rows) & (iota((rows, cols), 1) < 2 * rows)
    for slot, which in ((0, 4), (1, 1)):
        big = jnp.where(same, exact(exact(pick, st[which]), pick_t), 0.0)
        hi = big.astype(BF16).astype(F32)
        my[slot * rows:(slot + 1) * rows, :] = jnp.where(middle, big - hi, hi).astype(BF16)
    cols = 6 * count
    tile = ((iota((count, cols), 1) & (count - 1)) == iota((count, cols), 0)).astype(F32)
    stiff = exact(st[0], tile)
    mass = exact(st[3], tile)
    block = iota((count, cols), 1) >> 5
    big = jnp.where(block < 3, stiff, mass)
    hi = big.astype(BF16).astype(F32)
    mx[...] = jnp.where((block == 1) | (block == 4), big - hi, hi).astype(BF16)


def apply_patch(u, mx, my, mz):
    count, area = u.shape
    ni, nt = count // SUB, area // LANES
    tiles = jnp.concatenate(
        [u[SUB * i:SUB * (i + 1), LANES * t:LANES * (t + 1)] for i in range(ni) for t in range(nt)], axis=0
    )
    tiles = swap(tiles.reshape(ni * nt, SUB, LANES)).reshape(ni * nt * SUB, LANES)
    hi, lo = split(tiles)
    z = mul(jnp.concatenate([hi, lo, hi], axis=1), mz)
    rows = nt * SUB
    packed = []
    for slot in range(2):
        part = z[:, slot * LANES:(slot + 1) * LANES]
        wide = jnp.concatenate([part[rows * i:rows * (i + 1)] for i in range(ni)], axis=1)
        hi, lo = split(wide)
        packed.append(jnp.concatenate([hi, hi, lo], axis=0))
    both = mul(my, packed[0])
    first = both[:rows]
    second = both[rows:] + mul(my[:rows], packed[1])
    pieces = []
    for term in (first, second):
        stacked = jnp.concatenate([term[:, LANES * i:LANES * (i + 1)] for i in range(ni)], axis=0)
        stacked = swap(stacked.reshape(ni * nt, SUB, LANES))
        back = jnp.concatenate(
            [jnp.concatenate([stacked[i * nt + t] for i in range(ni)], axis=0) for t in range(nt)], axis=1
        )
        hi, lo = split(back)
        pieces += [hi, hi, lo]
    return mul(mx, jnp.concatenate(pieces, axis=0))


def kernel(sizes, start, st, basis, coef, mx, my, mz, wt, v0, field,
           zs, zr, xs, xr, ys, yr, es, er, rows, hsend, hrecv, rsend, rrecv, ready, locals_, images):
    nx, ny, nz = sizes
    total = nx * ny * nz
    count, area = start.shape
    nt = area // LANES
    ni = count // SUB
    last = count - 1
    px, py, pz = lax.axis_index("gx"), lax.axis_index("gy"), lax.axis_index("gz")
    me = (px * ny + py) * nz + pz
    coords = (px, py, pz)
    there = [[coords[d] > 0, coords[d] < sizes[d] - 1] for d in range(3)]

    for ref in (zr, xr, yr, er):
        ref[...] = jnp.zeros_like(ref)
    barrier = pltpu.get_barrier_semaphore()

    def peer(k):
        p = lax.rem(me + k, total)
        return (p // (ny * nz), (p // nz) % ny, p % nz)

    def every_peer(act):
        if total > 64:
            def step(k, carry):
                act(peer(k))
                return carry

            lax.fori_loop(1, total, step, 0)
            return
        around = [[lax.rem(coords[d] + k, sizes[d]) if k else coords[d] for k in range(sizes[d])] for d in range(3)]
        for ky in range(ny - 1, -1, -1):
            for kx in range(nx - 1, -1, -1):
                for kz in range(nz):
                    if kx or ky or kz:
                        act((around[0][kx], around[1][ky], around[2][kz]))

    def neighbours(act):
        for dx in (-1, 0, 1):
            for dy in (-1, 0, 1):
                for dz in (-1, 0, 1):
                    if dx or dy or dz:
                        target = (px + dx, py + dy, pz + dz)
                        inside = None
                        for d, step in enumerate((dx, dy, dz)):
                            if step:
                                side = there[d][(step + 1) // 2]
                                inside = side if inside is None else inside & side

                        @pl.when(inside)
                        def _():
                            act(target)

    around_me = 1
    for d in range(3):
        around_me = around_me * (1 + (coords[d] > 0).astype(jnp.int32) + (coords[d] < sizes[d] - 1).astype(jnp.int32))
    around_me = around_me - 1

    rounds = max(sizes) - 2

    def call(r):
        neighbours(lambda target: pl.semaphore_signal(ready.at[r], inc=1, device_id=target, device_id_type=MESH))

    neighbours(lambda target: pl.semaphore_signal(barrier, inc=1, device_id=target, device_id_type=MESH))

    def shared(index, d):
        return ((index == 0) & there[d][0]) | ((index == last) & there[d][1])

    lane = iota((count, area), 1)
    ia, ib, ic = iota((count, area), 0), lane >> 5, lane & (count - 1)
    half = lambda index, d: jnp.where(shared(index, d), 0.5, 1.0)
    weight = half(ia, 0) * half(ib, 1) * half(ic, 2)
    wt[...] = weight.astype(F32)
    field[...] = start[...] * wt[...]

    lane_c = iota((count, LANES), 1)
    face_c = (lane_c & (count - 1) == 0) | (lane_c & (count - 1) == last)
    even = (lane_c & 1) == 0
    lane8 = iota((SUB, LANES), 1)
    low8, high8 = lane8 < count, lane8 >= LANES - count
    lane1 = iota((1, LANES), 1)
    diag = iota((SUB, LANES), 0) == lane8

    def tile(t):
        return slice(t * LANES, (t + 1) * LANES)

    def halo_copies(phase):
        out = []

        def add(src, dst, slot, *direction):
            there_all, target = None, {}
            for d, step in enumerate(direction):
                if step is not None:
                    there_all = there[d][step] if there_all is None else there_all & there[d][step]
            target = tuple(c if step is None else c + 2 * step - 1 for c, step in zip(coords, direction))
            copy = pltpu.make_async_remote_copy(
                src_ref=src, dst_ref=dst.at[phase, slot], send_sem=hsend.at[phase, len(out)],
                recv_sem=hrecv.at[phase, len(out)], device_id=target, device_id_type=MESH)
            out.append((copy, there_all, direction, dst, slot))

        for z in (1, 0, None):
            for d in range(2):
                for e in range(2):
                    back = 0 if z is None else 2 - z
                    add(es.at[phase, 2 * d + e], er, (2 * (1 - d) + 1 - e) * 3 + back, d, e, z)
        for z in (1, 0, None):
            back = 0 if z is None else 2 - z
            for d in range(2):
                add(xs.at[phase, d], xr, (1 - d) * 3 + back, d, None, z)
        for z in (1, 0, None):
            back = 0 if z is None else 2 - z
            for d in range(2):
                add(ys.at[phase, d], yr, (1 - d) * 3 + back, None, d, z)
        for d in range(2):
            add(zs.at[phase], zr, 1 - d, None, None, d)
        return out

    def start_all(copies):
        for copy, exists, *_ in copies:
            @pl.when(exists)
            def _():
                copy.start()

    def send_halo(phase):
        copies = halo_copies(phase)
        for d in range(2):
            row = 0 if d == 0 else last
            for e in range(2):
                es[phase, 2 * d + e] = field[row:row + 1, tile(0 if e == 0 else nt - 1)]
            for t in range(nt):
                xs[phase, d, t:t + 1, :] = field[row:row + 1, tile(t)]
            packed = None
            for i in range(ni):
                block = field[SUB * i:SUB * (i + 1), tile(0 if d == 0 else nt - 1)]
                part = jnp.where(low8 if d == 0 else high8, block, 0.0)
                shift = (count * i + d * count) % LANES
                part = part if shift == 0 else pltpu.roll(part, shift, 1)
                packed = part if packed is None else packed + part
            ys[phase, d] = packed
        packed = None
        for t in range(nt):
            part = jnp.where(face_c, field[:, tile(t)], 0.0)
            part = part if t == 0 else pltpu.roll(part, 2 * t, 1)
            packed = part if packed is None else packed + part
        zs[phase] = packed
        start_all(copies)

    def fold(ref, phase, base):
        low = ref[phase, base + 1]
        c = iota(low.shape, 1) & (count - 1)
        out = ref[phase, base] + jnp.where(c == 0, pltpu.roll(low, LANES - last, 1), 0.0)
        return out + jnp.where(c == last, pltpu.roll(ref[phase, base + 2], last, 1), 0.0)

    def add_halo(phase):
        copies = halo_copies(phase)
        for index, (copy, _, direction, dst, slot) in enumerate(copies):
            mirror = None
            for d, step in enumerate(direction):
                if step is not None:
                    mirror = there[d][1 - step] if mirror is None else mirror & there[d][1 - step]

            @pl.when(mirror)
            def _():
                into = dst.at[phase, slot]
                pltpu.make_async_copy(into, into, hrecv.at[phase, index]).wait()
        merged = jnp.where(even, pltpu.roll(zr[phase, 0], LANES - last, 1), pltpu.roll(zr[phase, 1], last, 1))
        for t in range(nt):
            part = merged if t == 0 else pltpu.roll(merged, LANES - 2 * t, 1)
            field[:, tile(t)] += jnp.where(face_c, part, 0.0)
        for d in range(2):
            received = fold(yr, phase, 3 * d)
            for i in range(ni):
                shift = (-count * i - d * count) % LANES
                part = received if shift == 0 else pltpu.roll(received, shift, 1)
                field[SUB * i:SUB * (i + 1), tile(0 if d == 0 else nt - 1)] += jnp.where(low8 if d == 0 else high8, part, 0.0)
        for d in range(2):
            row = 0 if d == 0 else last
            received = fold(xr, phase, 3 * d)
            for t in range(nt):
                line = received[t:t + 1]
                if t == 0:
                    line += jnp.where(lane1 < count, pltpu.roll(fold(er, phase, 6 * d), count, 1), 0.0)
                if t == nt - 1:
                    line += jnp.where(lane1 >= LANES - count, pltpu.roll(fold(er, phase, 6 * d + 3), LANES - count, 1), 0.0)
                field[row:row + 1, tile(t)] += line

    def send_dots(phase, products):
        packed = None
        for k, product in enumerate(products):
            acc = None
            for i in range(ni):
                for t in range(nt):
                    block = product[SUB * i:SUB * (i + 1), tile(t)]
                    acc = block if acc is None else acc + block
            line = jnp.where(iota((SUB, LANES), 0) == k, jnp.sum(acc, axis=0, keepdims=True), 0.0)
            packed = line if packed is None else packed + line
        sums = jnp.sum(packed, axis=1, keepdims=True)
        rows[phase, me] = jnp.sum(jnp.where(diag, sums, 0.0), axis=0, keepdims=True)

        def send(target):
            pltpu.make_async_remote_copy(
                src_ref=rows.at[phase, me], dst_ref=rows.at[phase, me], send_sem=rsend.at[phase],
                recv_sem=rrecv.at[phase], device_id=target, device_id_type=MESH).start()

        every_peer(send)

    def take_dots(phase):
        others = rows.at[phase, pl.ds(0, total - 1)]
        pltpu.make_async_copy(others, others, rrecv.at[phase]).wait()
        line = jnp.sum(rows[phase], axis=0)
        return jnp.sum(jnp.where(diag, line, 0.0), axis=1, keepdims=True)

    build_matrices(st, mx, my, mz)
    pl.semaphore_wait(barrier, around_me)
    send_halo(0)
    for r in range(rounds):
        call(r)
        if r < rounds - 1:
            pl.semaphore_wait(ready.at[r], around_me)
    add_halo(0)
    vector = field[...]
    alpha = None
    row2, col2 = iota(coef.shape[1:], 0), iota(coef.shape[1:], 1)
    coefs = jnp.zeros(coef.shape[1:], F32)
    local = apply_patch(vector, mx[...], my[...], mz[...])
    field[...] = local
    send_halo(1)
    if rounds > 0:
        pl.semaphore_wait(ready.at[rounds - 1], around_me)
    send_dots(1, [wt[...] * vector * vector, local * vector])
    add_halo(1)
    image = field[...]
    for j in range(ITERS):
        more = j < ITERS - 1
        if more:
            ahead = apply_patch(image, mx[...], my[...], mz[...])
            field[...] = ahead
            send_halo(j + 2)
        sums = take_dots(j + 1)
        norm = jnp.sqrt(sums[0:1])
        inverse = 1.0 / norm
        if j > 0:
            coefs = jnp.where((row2 == 1) & (col2 == j - 1), norm * alpha, coefs)
        alpha = sums[1:2] / sums[0:1]
        coefs = jnp.where((row2 == 0) & (col2 == j), alpha, coefs)
        factor = inverse / alpha
        heights = [sums[2 + i:3 + i] * factor for i in range(j)]

        def follow(applied, unit, old):
            out = applied * factor - unit
            for i in range(j):
                out = out - heights[i] * old(i)
            return out

        old_vector = lambda i: v0[...] if i == 0 else basis[i - 1]
        unit = vector * inverse
        if j == 0:
            v0[...] = unit
        else:
            basis[j - 1] = unit
        vector = follow(image, unit, old_vector)
        if more:
            unit = local * inverse
            locals_[j] = unit
            local = follow(ahead, unit, lambda i: locals_[i])
            send_dots(j + 2, [wt[...] * vector * vector, local * vector] + [local * old_vector(i) for i in range(j + 1)])
            unit = image * inverse
            images[j] = unit
            add_halo(j + 2)
            image = follow(field[...], unit, lambda i: images[i])
    send_dots(ITERS + 1, [wt[...] * vector * vector])
    sums = take_dots(ITERS + 1)
    norm = jnp.sqrt(sums[0:1])
    coefs = jnp.where((row2 == 1) & (col2 == ITERS - 1), norm * alpha, coefs)
    basis[ITERS - 1] = vector * (1.0 / norm)
    coef[0] = coefs

    for phase in range(ITERS + 1):
        for copy, exists, *_ in halo_copies(phase):
            @pl.when(exists)
            def _():
                copy.wait_send()
    for phase in range(1, ITERS + 2):
        others = rows.at[phase, pl.ds(0, total - 1)]
        pltpu.make_async_copy(others, others, rsend.at[phase]).wait()


def shards(sizes, start, stencils):
    probes, count, area = start.shape[3:]
    nt = area // LANES
    total = sizes[0] * sizes[1] * sizes[2]
    halos = ITERS + 1
    vmem = pl.BlockSpec(memory_space=pltpu.VMEM)
    call = pl.pallas_call(
        functools.partial(kernel, sizes),
        out_shape=(jax.ShapeDtypeStruct((ITERS, count, area), F32), jax.ShapeDtypeStruct((1, 2, ITERS), F32)),
        in_specs=[vmem, vmem],
        out_specs=(vmem, vmem),
        scratch_shapes=[
            pltpu.VMEM((count, 6 * count), BF16),
            pltpu.VMEM((4 * count, 6 * count), BF16),
            pltpu.VMEM((3 * LANES, 2 * LANES), BF16),
            pltpu.VMEM((count, area), F32),
            pltpu.VMEM((count, area), F32),
            pltpu.VMEM((count, area), F32),
            pltpu.VMEM((halos, count, LANES), F32),
            pltpu.VMEM((halos, 2, count, LANES), F32),
            pltpu.VMEM((halos, 2, nt, LANES), F32),
            pltpu.VMEM((halos, 6, nt, LANES), F32),
            pltpu.VMEM((halos, 2, SUB, LANES), F32),
            pltpu.VMEM((halos, 6, SUB, LANES), F32),
            pltpu.VMEM((halos, 4, 1, LANES), F32),
            pltpu.VMEM((halos, 12, 1, LANES), F32),
            pltpu.VMEM((halos + 1, total, 1, LANES), F32),
            pltpu.SemaphoreType.DMA((halos, 26)),
            pltpu.SemaphoreType.DMA((halos, 26)),
            pltpu.SemaphoreType.DMA((halos + 1,)),
            pltpu.SemaphoreType.DMA((halos + 1,)),
            pltpu.SemaphoreType.REGULAR((max(1, max(sizes) - 2),)),
            pltpu.VMEM((ITERS - 1, count, area), F32),
            pltpu.VMEM((ITERS - 1, count, area), F32),
        ],
        compiler_params=pltpu.CompilerParams(collective_id=0, has_side_effects=True, vmem_limit_bytes=48 * 1024 * 1024),
    )
    results = [call(start[0, 0, 0, p], stencils[:, 0, 0, 0]) for p in range(probes)]
    basis = jnp.stack([r[0] for r in results])
    return basis[None, None, None], jnp.concatenate([r[1] for r in results])


def solution(mesh):
    sizes = tuple(mesh.shape[name] for name in ("gx", "gy", "gz"))
    return jax.shard_map(
        functools.partial(shards, sizes),
        mesh=mesh,
        in_specs=(P("gx", "gy", "gz", None, None, None), P(None, "gx", "gy", "gz", None, None)),
        out_specs=(P("gx", "gy", "gz", None, None, None, None), P()),
        check_vma=False,
    )
```

profile of v0, /device:TPU:0, one launch (start us, length us, event | category | flops | bytes accessed | tf_op | source)
XLA Modules:
  0.0 46.0 jit_solution(5688140069459818037)
XLA Ops:
  0.6 0.0 copy-start
  0.6 0.9 %copy-done = f32[1,1,1,1,32,1024]{5,4,3,2,1,0:T(8,128)S(1)} copy-done((f32[1,1,1,1,32,1024]{5,4,3,2,1,0:T(8,128)S(1)}, f32[1,1,1,1,32,1024]{5,4,3,2,1,0:T(8,128)}, u32[]{:S(2)}) %copy-start) | copy-done | bytes 131096
  1.5 0.0 copy-start.1
  1.5 0.9 %copy-done.1 = f32[6,1,1,1,32,32]{5,4,3,2,1,0:T(8,128)S(1)} copy-done((f32[6,1,1,1,32,32]{5,4,3,2,1,0:T(8,128)S(1)}, f32[6,1,1,1,32,32]{5,4,3,2,1,0:T(8,128)}, u32[]{:S(2)}) %copy-start.1) | copy-done | bytes 24600
  2.4 42.2 %shard_map.41 = (f32[5,32,1024]{2,1,0:T(8,128)S(1)}, f32[1,2,5]{2,1,0:T(2,128)S(1)}) custom-call(f32[32,1024]{1,0:T(8,128)S(1)} %bitcast.4, f32[6,32,32]{2,1,0:T(8,128)S(1)} %bitcast.5), custom_call_target="tpu_custom_call" | custom-call | tf_op jit(solution)/shard_map/pallas_call | solution.py:436
  44.6 0.8 %copy.6 = f32[1,1,1,1,5,32,1024]{6,5,4,3,2,1,0:T(8,128)} copy(f32[1,1,1,1,5,32,1024]{6,5,4,3,2,1,0:T(8,128)S(1)} %bitcast.3) | data formatting | bytes 1310720
  45.4 0.6 %copy.7 = f32[1,2,5]{2,1,0:T(2,128)} copy(f32[1,2,5]{2,1,0:T(2,128)S(1)} %get-tuple-element.9) | data formatting | bytes 80
Async XLA Ops:
  0.6 0.9 %copy-start = (f32[1,1,1,1,32,1024]{5,4,3,2,1,0:T(8,128)S(1)}, f32[1,1,1,1,32,1024]{5,4,3,2,1,0:T(8,128)}, u32[]{:S(2)}) copy-start(f32[1,1,1,1,32,1024]{5,4,3,2,1,0:T(8,128)} %param.2) | copy-start | bytes 393220
  1.5 0.9 %copy-start.1 = (f32[6,1,1,1,32,32]{5,4,3,2,1,0:T(8,128)S(1)}, f32[6,1,1,1,32,32]{5,4,3,2,1,0:T(8,128)}, u32[]{:S(2)}) copy-start(f32[6,1,1,1,32,32]{5,4,3,2,1,0:T(8,128)} %param.3) | copy-start | bytes 73732
where the time goes:
time: 46.2 us; the launch traced here: 46 us
  Pallas kernels  42.2 us (91%)
  local copies, waits for them, and re-layouts  3.19 us (7%)
  between operations  0.65 us (1%)
    pallas_call x1, Pallas kernels, shards(): call(start[0, 0, 0, p], stencils[:, 0, 0, 0])  42.2 us
    unnamed x6, local copies, waits for them, and re-layouts  3.19 us

commit v1 on v0

--- a/solution.py
+++ b/solution.py
@@ -110,8 +110,12 @@
     return mul(mx, jnp.concatenate(pieces, axis=0))
 
 
-def kernel(sizes, start, st, basis, coef, mx, my, mz, wt, v0, field,
-           zs, zr, xs, xr, ys, yr, es, er, rows, hsend, hrecv, rsend, rrecv, ready, locals_, images):
+def kernel(sizes, start_in, st_in, basis, coef, mx, my, mz, wt, v0, field,
+           zs, zr, xs, xr, ys, yr, es, er, rows, hsend, hrecv, rsend, rrecv, ready, locals_, images, start, st, loads):
+    load_start = pltpu.make_async_copy(start_in, start, loads.at[0])
+    load_st = pltpu.make_async_copy(st_in, st, loads.at[1])
+    load_start.start()
+    load_st.start()
     nx, ny, nz = sizes
     total = nx * ny * nz
     count, area = start.shape
@@ -182,6 +186,7 @@
     half = lambda index, d: jnp.where(shared(index, d), 0.5, 1.0)
     weight = half(ia, 0) * half(ib, 1) * half(ic, 2)
     wt[...] = weight.astype(F32)
+    load_start.wait()
     field[...] = start[...] * wt[...]
 
     lane_c = iota((count, LANES), 1)
@@ -321,9 +326,10 @@
         line = jnp.sum(rows[phase], axis=0)
         return jnp.sum(jnp.where(diag, line, 0.0), axis=1, keepdims=True)
 
-    build_matrices(st, mx, my, mz)
     pl.semaphore_wait(barrier, around_me)
     send_halo(0)
+    load_st.wait()
+    build_matrices(st, mx, my, mz)
     for r in range(rounds):
         call(r)
         if r < rounds - 1:
@@ -396,16 +402,26 @@
         pltpu.make_async_copy(others, others, rsend.at[phase]).wait()
 
 
+def store(basis, coef, basis_out, coef_out, sems):
+    copies = [pltpu.make_async_copy(basis.at[i], basis_out.at[i], sems.at[i]) for i in range(ITERS)]
+    copies.append(pltpu.make_async_copy(coef, coef_out, sems.at[ITERS]))
+    for copy in copies:
+        copy.start()
+    for copy in copies:
+        copy.wait()
+
+
 def shards(sizes, start, stencils):
     probes, count, area = start.shape[3:]
     nt = area // LANES
     total = sizes[0] * sizes[1] * sizes[2]
     halos = ITERS + 1
     vmem = pl.BlockSpec(memory_space=pltpu.VMEM)
+    call_shapes = (jax.ShapeDtypeStruct((ITERS, count, area), F32), jax.ShapeDtypeStruct((1, 2, ITERS), F32))
     call = pl.pallas_call(
         functools.partial(kernel, sizes),
-        out_shape=(jax.ShapeDtypeStruct((ITERS, count, area), F32), jax.ShapeDtypeStruct((1, 2, ITERS), F32)),
-        in_specs=[vmem, vmem],
+        out_shape=call_shapes,
+        in_specs=[pl.BlockSpec(memory_space=pltpu.HBM)] * 2,
         out_specs=(vmem, vmem),
         scratch_shapes=[
             pltpu.VMEM((count, 6 * count), BF16),
@@ -430,10 +446,22 @@
             pltpu.SemaphoreType.REGULAR((max(1, max(sizes) - 2),)),
             pltpu.VMEM((ITERS - 1, count, area), F32),
             pltpu.VMEM((ITERS - 1, count, area), F32),
+            pltpu.VMEM((count, area), F32),
+            pltpu.VMEM(stencils.shape[:1] + stencils.shape[4:], F32),
+            pltpu.SemaphoreType.DMA((2,)),
         ],
         compiler_params=pltpu.CompilerParams(collective_id=0, has_side_effects=True, vmem_limit_bytes=48 * 1024 * 1024),
     )
-    results = [call(start[0, 0, 0, p], stencils[:, 0, 0, 0]) for p in range(probes)]
+    hbm = pl.BlockSpec(memory_space=pltpu.HBM)
+    put = pl.pallas_call(
+        store,
+        out_shape=call_shapes,
+        in_specs=[vmem, vmem],
+        out_specs=(hbm, hbm),
+        scratch_shapes=[pltpu.SemaphoreType.DMA((ITERS + 1,))],
+        compiler_params=pltpu.CompilerParams(vmem_limit_bytes=4 * 1024 * 1024),
+    )
+    results = [put(*call(*(pltpu.with_memory_space_constraint(x, pltpu.HBM) for x in (start[0, 0, 0, p], stencils[:, 0, 0, 0])))) for p in range(probes)]
     basis = jnp.stack([r[0] for r in results])
     return basis[None, None, None], jnp.concatenate([r[1] for r in results])
 

time: 46.2 us -> 43.8 us (0.948)
  local copies, waits for them, and re-layouts: 3.19 us -> 0 us
  Pallas kernels: 42.2 us -> 43.1 us
    unnamed x6 -> x0, local copies, waits for them, and re-layouts: 3.19 us -> none
    pallas_call x1 -> x2, Pallas kernels: 42.2 us -> 43.1 us  [the longest x1 42.2 us: shards(): call(*(pltpu.with_memory_space_constraint(x, pltpu.HBM) for x in (start[0...]
where the time goes in v1:
time: 43.8 us; the launch traced here: 43.7 us
  Pallas kernels  43.1 us (98%)
  between operations  0.64 us (1%)
    pallas_call x1, Pallas kernels, shards(): call(*(pltpu.with_memory_space_constraint(x, pltpu.HBM) for x in (start[0...  42.2 us
    pallas_call x1, Pallas kernels, shards(): put(*call(*(pltpu.with_memory_space_constraint(x, pltpu.HBM) for x in (st...  0.88 us

profile of v1, /device:TPU:0, one launch (start us, length us, event | category | flops | bytes accessed | tf_op | source)
XLA Modules:
  0.0 43.7 jit_solution(13195685787865920583)
XLA Ops:
  0.6 42.2 %shard_map.41 = (f32[5,32,1024]{2,1,0:T(8,128)S(1)}, f32[1,2,5]{2,1,0:T(2,128)S(1)}) custom-call(f32[32,1024]{1,0:T(8,128)} %bitcast.3, f32[6,32,32]{2,1,0:T(8,128)} %bitcast.4), custom_call_target="tpu_custom_call" | custom-call | tf_op jit(solution)/shard_map/pallas_call | solution.py:464
  42.8 0.9 %shard_map.42 = (f32[5,32,1024]{2,1,0:T(8,128)}, f32[1,2,5]{2,1,0:T(2,128)}) custom-call(f32[5,32,1024]{2,1,0:T(8,128)S(1)} %get-tuple-element.6.basis, f32[1,2,5]{2,1,0:T(2,128)S(1)} %get-tuple-element.7.coef), custom_call_target="tpu_custom_call" | custom-call | tf_op jit(solution)/shard_map/pallas_call | solution.py:464

commit v2 on v1

--- a/solution.py
+++ b/solution.py
@@ -34,15 +34,14 @@
 
 
 def swap(x):
-    sub = iota((1, SUB, LANES), 1)
-    group = iota((1, SUB, LANES), 2) >> 5
-    s0, s1 = sub & 1, (sub >> 1) & 1
-    g0, g1 = group & 1, (group >> 1) & 1
-    far = pltpu.roll(x, 64, 2)
-    x = jnp.where(s1 == g1, x, jnp.where(s1 == 0, pltpu.roll(far, SUB - 2, 1), pltpu.roll(far, 2, 1)))
-    up = pltpu.roll(pltpu.roll(x, SUB - 1, 1), 32, 2)
-    down = pltpu.roll(pltpu.roll(x, 1, 1), LANES - 32, 2)
-    return jnp.where(s0 == g0, x, jnp.where(s0 == 0, up, down))
+    sub = iota((1, SUB, LANES), 1) & 3
+    apart = ((iota((1, SUB, LANES), 2) >> 5) - sub) & 3
+    out = x
+    for d in range(1, 4):
+        far = pltpu.roll(x, 32 * d, 2)
+        moved = jnp.where(sub < 4 - d, pltpu.roll(far, SUB - d, 1), pltpu.roll(far, 4 - d, 1))
+        out = jnp.where(apart == d, moved, out)
+    return out
 
 
 def build_matrices(st, mx, my, mz):
@@ -110,8 +109,8 @@
     return mul(mx, jnp.concatenate(pieces, axis=0))
 
 
-def kernel(sizes, start_in, st_in, basis, coef, mx, my, mz, wt, v0, field,
-           zs, zr, xs, xr, ys, yr, es, er, rows, hsend, hrecv, rsend, rrecv, ready, locals_, images, start, st, loads):
+def kernel(sizes, start_in, st_in, basis, coef, mx, my, mz, wt, field,
+           zs, zr, xs, xr, ys, yr, es, er, rows, hsend, hrecv, rsend, rrecv, ready, ws, start, st, loads):
     load_start = pltpu.make_async_copy(start_in, start, loads.at[0])
     load_st = pltpu.make_async_copy(st_in, st, loads.at[1])
     load_start.start()
@@ -214,16 +213,16 @@
                 recv_sem=hrecv.at[phase, len(out)], device_id=target, device_id_type=MESH)
             out.append((copy, there_all, direction, dst, slot))
 
-        for z in (1, 0, None):
+        for z in (None, 1, 0):
             for d in range(2):
                 for e in range(2):
                     back = 0 if z is None else 2 - z
                     add(es.at[phase, 2 * d + e], er, (2 * (1 - d) + 1 - e) * 3 + back, d, e, z)
-        for z in (1, 0, None):
+        for z in (None, 1, 0):
             back = 0 if z is None else 2 - z
             for d in range(2):
                 add(xs.at[phase, d], xr, (1 - d) * 3 + back, d, None, z)
-        for z in (1, 0, None):
+        for z in (None, 1, 0):
             back = 0 if z is None else 2 - z
             for d in range(2):
                 add(ys.at[phase, d], yr, (1 - d) * 3 + back, None, d, z)
@@ -261,11 +260,12 @@
         zs[phase] = packed
         start_all(copies)
 
-    def fold(ref, phase, base):
+    def fold(ref, phase, base, shift=0):
         low = ref[phase, base + 1]
         c = iota(low.shape, 1) & (count - 1)
-        out = ref[phase, base] + jnp.where(c == 0, pltpu.roll(low, LANES - last, 1), 0.0)
-        return out + jnp.where(c == last, pltpu.roll(ref[phase, base + 2], last, 1), 0.0)
+        turn = lambda x, by: x if by % LANES == 0 else pltpu.roll(x, by % LANES, 1)
+        out = turn(ref[phase, base], shift) + jnp.where(c == 0, turn(low, shift - last), 0.0)
+        return out + jnp.where(c == last, turn(ref[phase, base + 2], shift + last), 0.0)
 
     def add_halo(phase):
         copies = halo_copies(phase)
@@ -295,9 +295,9 @@
             for t in range(nt):
                 line = received[t:t + 1]
                 if t == 0:
-                    line += jnp.where(lane1 < count, pltpu.roll(fold(er, phase, 6 * d), count, 1), 0.0)
+                    line += jnp.where(lane1 < count, fold(er, phase, 6 * d, count), 0.0)
                 if t == nt - 1:
-                    line += jnp.where(lane1 >= LANES - count, pltpu.roll(fold(er, phase, 6 * d + 3), LANES - count, 1), 0.0)
+                    line += jnp.where(lane1 >= LANES - count, fold(er, phase, 6 * d + 3, LANES - count), 0.0)
                 field[row:row + 1, tile(t)] += line
 
     def send_dots(phase, products):
@@ -335,61 +335,74 @@
         if r < rounds - 1:
             pl.semaphore_wait(ready.at[r], around_me)
     add_halo(0)
-    vector = field[...]
-    alpha = None
+    ws[0] = field[...]
+    gram, rho = {}, [None]
+
+    def gather(k):
+        sums = take_dots(k)
+        for i in range(k + 1):
+            gram[i, k] = sums[i:i + 1]
+        if k < ITERS:
+            rho.append(sums[k + 1:k + 2] / sums[k:k + 1])
+
+    for k in range(ITERS):
+        vector = ws[k]
+        local = apply_patch(vector, mx[...], my[...], mz[...])
+        field[...] = local
+        send_halo(k + 1)
+        if k == 0 and rounds > 0:
+            pl.semaphore_wait(ready.at[rounds - 1], around_me)
+        weighted = wt[...] * vector
+        send_dots(k, [weighted * ws[i] for i in range(k + 1)] + [local * vector])
+        if k > 0:
+            gather(k - 1)
+        add_halo(k + 1)
+        ws[k + 1] = field[...] if k == 0 else field[...] * (1.0 / rho[k]) - vector
+    weighted = wt[...] * ws[ITERS]
+    send_dots(ITERS, [weighted * ws[i] for i in range(ITERS + 1)])
+    gather(ITERS - 1)
+
+    upper, inverse, scale = {}, {}, []
+
+    def column(k):
+        for i in range(k):
+            total_i = None
+            for m in range(i + 1):
+                term = inverse[m, i] * gram[m, k]
+                total_i = term if total_i is None else total_i + term
+            upper[i, k] = total_i
+        rest = gram[k, k]
+        for i in range(k):
+            rest = rest - upper[i, k] * upper[i, k]
+        upper[k, k] = jnp.sqrt(rest)
+        inverse[k, k] = 1.0 / upper[k, k]
+        for i in range(k):
+            total_i = None
+            for m in range(i, k):
+                term = inverse[i, m] * upper[m, k]
+                total_i = term if total_i is None else total_i + term
+            inverse[i, k] = -total_i * inverse[k, k]
+        if k > 0:
+            out = ws[0] * inverse[0, k]
+            for i in range(1, k + 1):
+                out = out + ws[i] * inverse[i, k]
+            basis[k - 1] = out
+
+    for k in range(ITERS):
+        column(k)
+    gather(ITERS)
+    column(ITERS)
     row2, col2 = iota(coef.shape[1:], 0), iota(coef.shape[1:], 1)
     coefs = jnp.zeros(coef.shape[1:], F32)
-    local = apply_patch(vector, mx[...], my[...], mz[...])
-    field[...] = local
-    send_halo(1)
-    if rounds > 0:
-        pl.semaphore_wait(ready.at[rounds - 1], around_me)
-    send_dots(1, [wt[...] * vector * vector, local * vector])
-    add_halo(1)
-    image = field[...]
-    for j in range(ITERS):
-        more = j < ITERS - 1
-        if more:
-            ahead = apply_patch(image, mx[...], my[...], mz[...])
-            field[...] = ahead
-            send_halo(j + 2)
-        sums = take_dots(j + 1)
-        norm = jnp.sqrt(sums[0:1])
-        inverse = 1.0 / norm
-        if j > 0:
-            coefs = jnp.where((row2 == 1) & (col2 == j - 1), norm * alpha, coefs)
-        alpha = sums[1:2] / sums[0:1]
-        coefs = jnp.where((row2 == 0) & (col2 == j), alpha, coefs)
-        factor = inverse / alpha
-        heights = [sums[2 + i:3 + i] * factor for i in range(j)]
-
-        def follow(applied, unit, old):
-            out = applied * factor - unit
-            for i in range(j):
-                out = out - heights[i] * old(i)
-            return out
-
-        old_vector = lambda i: v0[...] if i == 0 else basis[i - 1]
-        unit = vector * inverse
-        if j == 0:
-            v0[...] = unit
-        else:
-            basis[j - 1] = unit
-        vector = follow(image, unit, old_vector)
-        if more:
-            unit = local * inverse
-            locals_[j] = unit
-            local = follow(ahead, unit, lambda i: locals_[i])
-            send_dots(j + 2, [wt[...] * vector * vector, local * vector] + [local * old_vector(i) for i in range(j + 1)])
-            unit = image * inverse
-            images[j] = unit
-            add_halo(j + 2)
-            image = follow(field[...], unit, lambda i: images[i])
-    send_dots(ITERS + 1, [wt[...] * vector * vector])
-    sums = take_dots(ITERS + 1)
-    norm = jnp.sqrt(sums[0:1])
-    coefs = jnp.where((row2 == 1) & (col2 == ITERS - 1), norm * alpha, coefs)
-    basis[ITERS - 1] = vector * (1.0 / norm)
+    for k in range(ITERS):
+        step = 1.0 if k == 0 else rho[k]
+        alpha = step * (upper[k, k + 1] * inverse[k, k])
+        if k > 0:
+            alpha = alpha + rho[k]
+            alpha = alpha - (1.0 if k == 1 else rho[k - 1]) * (upper[k - 1, k] * inverse[k - 1, k - 1])
+        beta = step * (upper[k + 1, k + 1] * inverse[k, k])
+        coefs = jnp.where((row2 == 0) & (col2 == k), alpha, coefs)
+        coefs = jnp.where((row2 == 1) & (col2 == k), beta, coefs)
     coef[0] = coefs
 
     for phase in range(ITERS + 1):
@@ -397,7 +410,7 @@
             @pl.when(exists)
             def _():
                 copy.wait_send()
-    for phase in range(1, ITERS + 2):
+    for phase in range(ITERS + 1):
         others = rows.at[phase, pl.ds(0, total - 1)]
         pltpu.make_async_copy(others, others, rsend.at[phase]).wait()
 
@@ -429,7 +442,6 @@
             pltpu.VMEM((3 * LANES, 2 * LANES), BF16),
             pltpu.VMEM((count, area), F32),
             pltpu.VMEM((count, area), F32),
-            pltpu.VMEM((count, area), F32),
             pltpu.VMEM((halos, count, LANES), F32),
             pltpu.VMEM((halos, 2, count, LANES), F32),
             pltpu.VMEM((halos, 2, nt, LANES), F32),
@@ -438,14 +450,13 @@
             pltpu.VMEM((halos, 6, SUB, LANES), F32),
             pltpu.VMEM((halos, 4, 1, LANES), F32),
             pltpu.VMEM((halos, 12, 1, LANES), F32),
-            pltpu.VMEM((halos + 1, total, 1, LANES), F32),
+            pltpu.VMEM((halos, total, 1, LANES), F32),
             pltpu.SemaphoreType.DMA((halos, 26)),
             pltpu.SemaphoreType.DMA((halos, 26)),
-            pltpu.SemaphoreType.DMA((halos + 1,)),
-            pltpu.SemaphoreType.DMA((halos + 1,)),
+            pltpu.SemaphoreType.DMA((halos,)),
+            pltpu.SemaphoreType.DMA((halos,)),
             pltpu.SemaphoreType.REGULAR((max(1, max(sizes) - 2),)),
-            pltpu.VMEM((ITERS - 1, count, area), F32),
-            pltpu.VMEM((ITERS - 1, count, area), F32),
+            pltpu.VMEM((halos, count, area), F32),
             pltpu.VMEM((count, area), F32),
             pltpu.VMEM(stencils.shape[:1] + stencils.shape[4:], F32),
             pltpu.SemaphoreType.DMA((2,)),

time: 43.8 us -> 41.6 us (0.950)
  Pallas kernels: 43.1 us -> 40.8 us
    pallas_call x1, Pallas kernels: 42.2 us -> 39.9 us  [shards(): call(*(pltpu.with_memory_space_constraint(x, pltpu.HBM) for x in (start[0...]
where the time goes in v2:
time: 41.6 us; the launch traced here: 41.5 us
  Pallas kernels  40.8 us (98%)
  between operations  0.64 us (2%)
    pallas_call x1, Pallas kernels, shards(): call(*(pltpu.with_memory_space_constraint(x, pltpu.HBM) for x in (start[0...  39.9 us
    pallas_call x1, Pallas kernels, shards(): put(*call(*(pltpu.with_memory_space_constraint(x, pltpu.HBM) for x in (st...  0.88 us

profile of v2, /device:TPU:0, one launch (start us, length us, event | category | flops | bytes accessed | tf_op | source)
XLA Modules:
  0.0 41.5 jit_solution(3676006009148308780)
XLA Ops:
  0.6 39.9 %shard_map.41 = (f32[5,32,1024]{2,1,0:T(8,128)S(1)}, f32[1,2,5]{2,1,0:T(2,128)S(1)}) custom-call(f32[32,1024]{1,0:T(8,128)} %bitcast.3, f32[6,32,32]{2,1,0:T(8,128)} %bitcast.4), custom_call_target="tpu_custom_call" | custom-call | tf_op jit(solution)/shard_map/pallas_call | solution.py:475
  40.6 0.9 %shard_map.42 = (f32[5,32,1024]{2,1,0:T(8,128)}, f32[1,2,5]{2,1,0:T(2,128)}) custom-call(f32[5,32,1024]{2,1,0:T(8,128)S(1)} %get-tuple-element.6.basis, f32[1,2,5]{2,1,0:T(2,128)S(1)} %get-tuple-element.7.coef), custom_call_target="tpu_custom_call" | custom-call | tf_op jit(solution)/shard_map/pallas_call | solution.py:475

commit v3 on v2

--- a/solution.py
+++ b/solution.py
@@ -44,7 +44,7 @@
     return out
 
 
-def build_matrices(st, mx, my, mz):
+def build_matrices(st, mx, my, mz, mzt, ya, yb):
     count = st.shape[1]
     wide = LANES
     spread = ((iota((wide, count), 0) & (count - 1)) == iota((wide, count), 1)).astype(F32)
@@ -52,10 +52,11 @@
     same = (iota((wide, wide), 0) >> 5) == (iota((wide, wide), 1) >> 5)
     for slot, which in ((0, 5), (1, 2)):
         big = exact(exact(spread, st[which].T), spread_t)
-        hi, lo = split(jnp.where(same, big, 0.0))
-        mz[0:wide, slot * wide:(slot + 1) * wide] = hi
-        mz[wide:2 * wide, slot * wide:(slot + 1) * wide] = hi
-        mz[2 * wide:3 * wide, slot * wide:(slot + 1) * wide] = lo
+        for ref, values in ((mz, jnp.where(same, big, 0.0)), (mzt, big)):
+            hi, lo = split(values)
+            ref[0:wide, slot * wide:(slot + 1) * wide] = hi
+            ref[wide:2 * wide, slot * wide:(slot + 1) * wide] = hi
+            ref[2 * wide:3 * wide, slot * wide:(slot + 1) * wide] = lo
     rows = 2 * count
     r = iota((rows, count), 0)
     pick = (((r >> 3) * 4 + (r & 3)) == iota((rows, count), 1)).astype(F32)
@@ -68,48 +69,68 @@
         big = jnp.where(same, exact(exact(pick, st[which]), pick_t), 0.0)
         hi = big.astype(BF16).astype(F32)
         my[slot * rows:(slot + 1) * rows, :] = jnp.where(middle, big - hi, hi).astype(BF16)
-    cols = 6 * count
-    tile = ((iota((count, cols), 1) & (count - 1)) == iota((count, cols), 0)).astype(F32)
-    stiff = exact(st[0], tile)
-    mass = exact(st[3], tile)
-    block = iota((count, cols), 1) >> 5
-    big = jnp.where(block < 3, stiff, mass)
+    cols = 7 * count
+    row, col = iota((count, cols), 0), iota((count, cols), 1)
+    block, extra, part = col >> 5, col >= 6 * count, (col >> 3) & 3
+    source = jnp.where(extra, jnp.where((col & 2) == 0, 0, count - 1), col & (count - 1))
+    tile = (source == row).astype(F32)
+    big = jnp.where((extra & ((col & 4) == 0)) | (~extra & (block >= 3)), exact(st[3], tile), exact(st[0], tile))
     hi = big.astype(BF16).astype(F32)
-    mx[...] = jnp.where((block == 1) | (block == 4), big - hi, hi).astype(BF16)
-
-
-def apply_patch(u, mx, my, mz):
+    rest = (~extra & ((block == 1) | (block == 4))) | (extra & (part == 1))
+    mx[...] = jnp.where(extra & (part == 3), 0.0, jnp.where(rest, big - hi, hi)).astype(BF16)
+    r, b = iota((SUB, count), 0), iota((SUB, count), 1)
+    ends = (b == jnp.where((r & 1) == 0, 0, count - 1)).astype(F32)
+    area = ya.shape[1]
+    widen = ((iota((count, area), 1) >> 5) == iota((count, area), 0)).astype(F32)
+    mass = exact(exact(ends, st[4].T), widen)
+    stiff = exact(exact(ends, st[1].T), widen)
+    upper = iota((SUB, area), 0) < SUB // 2
+    ya[...] = jnp.where(upper, stiff, mass)
+    yb[...] = jnp.where(upper, mass, 0.0)
+
+
+def apply_patch(u, mx, my, mz, late, send):
     count, area = u.shape
     ni, nt = count // SUB, area // LANES
-    tiles = jnp.concatenate(
-        [u[SUB * i:SUB * (i + 1), LANES * t:LANES * (t + 1)] for i in range(ni) for t in range(nt)], axis=0
-    )
-    tiles = swap(tiles.reshape(ni * nt, SUB, LANES)).reshape(ni * nt * SUB, LANES)
-    hi, lo = split(tiles)
-    z = mul(jnp.concatenate([hi, lo, hi], axis=1), mz)
     rows = nt * SUB
-    packed = []
-    for slot in range(2):
-        part = z[:, slot * LANES:(slot + 1) * LANES]
-        wide = jnp.concatenate([part[rows * i:rows * (i + 1)] for i in range(ni)], axis=1)
-        hi, lo = split(wide)
-        packed.append(jnp.concatenate([hi, hi, lo], axis=0))
-    both = mul(my, packed[0])
-    first = both[:rows]
-    second = both[rows:] + mul(my[:rows], packed[1])
-    pieces = []
-    for term in (first, second):
-        stacked = jnp.concatenate([term[:, LANES * i:LANES * (i + 1)] for i in range(ni)], axis=0)
-        stacked = swap(stacked.reshape(ni * nt, SUB, LANES))
-        back = jnp.concatenate(
-            [jnp.concatenate([stacked[i * nt + t] for i in range(ni)], axis=0) for t in range(nt)], axis=1
-        )
-        hi, lo = split(back)
-        pieces += [hi, hi, lo]
-    return mul(mx, jnp.concatenate(pieces, axis=0))
-
-
-def kernel(sizes, start_in, st_in, basis, coef, mx, my, mz, wt, field,
+    terms = []
+    for h in range(2):
+        group = range(h * ni // 2, (h + 1) * ni // 2)
+        tiles = jnp.concatenate([u[SUB * i:SUB * (i + 1), LANES * t:LANES * (t + 1)] for i in group for t in range(nt)], axis=0)
+        tiles = swap(tiles.reshape(-1, SUB, LANES)).reshape(-1, LANES)
+        hi, lo = split(tiles)
+        z = mul(jnp.concatenate([hi, lo, hi], axis=1), mz)
+        packed = []
+        for slot in range(2):
+            part = z[:, slot * LANES:(slot + 1) * LANES]
+            wide = jnp.concatenate([part[rows * i:rows * (i + 1)] for i in range(len(group))], axis=1)
+            hi, lo = split(wide)
+            packed.append(jnp.concatenate([hi, hi, lo], axis=0))
+        both = mul(my, packed[0])
+        terms.append((both[:rows], both[rows:] + mul(my[:rows], packed[1])))
+    lines = late()
+    half = ni // 2
+    order = [0, nt - 1] + list(range(1, nt - 1))
+    for at in range(0, nt, 2):
+        pair = order[at:at + 2]
+        stacked = jnp.stack([
+            terms[i // half][k][SUB * t:SUB * (t + 1), LANES * (i % half):LANES * (i % half + 1)]
+            for k in range(2) for t in pair for i in range(ni)
+        ])
+        stacked = swap(stacked)
+        pieces = []
+        for k in range(2):
+            back = jnp.concatenate([
+                jnp.concatenate([stacked[(k * 2 + n) * ni + i] for i in range(ni)], axis=0) for n in range(2)
+            ], axis=1)
+            hi, lo = split(back)
+            pieces += [hi, hi, lo]
+        pieces.append(jnp.concatenate([lines[t] for t in pair], axis=1))
+        out = mul(mx, jnp.concatenate(pieces, axis=0))
+        send({t: out[:, LANES * n:LANES * (n + 1)] for n, t in enumerate(pair)}, at == 0)
+
+
+def kernel(sizes, start_in, st_in, basis, coef, mx, my, mz, mzt, ya, yb, wt, field,
            zs, zr, xs, xr, ys, yr, es, er, rows, hsend, hrecv, rsend, rrecv, ready, ws, start, st, loads):
     load_start = pltpu.make_async_copy(start_in, start, loads.at[0])
     load_st = pltpu.make_async_copy(st_in, st, loads.at[1])
@@ -202,32 +223,32 @@
     def halo_copies(phase):
         out = []
 
-        def add(src, dst, slot, *direction):
+        def add(src, into, *direction):
             there_all, target = None, {}
             for d, step in enumerate(direction):
                 if step is not None:
                     there_all = there[d][step] if there_all is None else there_all & there[d][step]
             target = tuple(c if step is None else c + 2 * step - 1 for c, step in zip(coords, direction))
             copy = pltpu.make_async_remote_copy(
-                src_ref=src, dst_ref=dst.at[phase, slot], send_sem=hsend.at[phase, len(out)],
+                src_ref=src, dst_ref=into, send_sem=hsend.at[phase, len(out)],
                 recv_sem=hrecv.at[phase, len(out)], device_id=target, device_id_type=MESH)
-            out.append((copy, there_all, direction, dst, slot))
+            out.append((copy, there_all, direction, into))
 
         for z in (None, 1, 0):
             for d in range(2):
                 for e in range(2):
                     back = 0 if z is None else 2 - z
-                    add(es.at[phase, 2 * d + e], er, (2 * (1 - d) + 1 - e) * 3 + back, d, e, z)
+                    add(es.at[phase, 2 * d + e], er.at[phase, back, pl.ds(2 * (1 - d) + 1 - e, 1)], d, e, z)
         for z in (None, 1, 0):
             back = 0 if z is None else 2 - z
             for d in range(2):
-                add(xs.at[phase, d], xr, (1 - d) * 3 + back, d, None, z)
+                add(xs.at[phase, d], xr.at[phase, (1 - d) * 3 + back], d, None, z)
         for z in (None, 1, 0):
             back = 0 if z is None else 2 - z
             for d in range(2):
-                add(ys.at[phase, d], yr, (1 - d) * 3 + back, None, d, z)
+                add(ys.at[phase, d], yr.at[phase, (1 - d) * 3 + back], None, d, z)
         for d in range(2):
-            add(zs.at[phase], zr, 1 - d, None, None, d)
+            add(zs.at[phase], zr.at[phase, 1 - d], None, None, d)
         return out
 
     def start_all(copies):
@@ -238,27 +259,41 @@
 
     def send_halo(phase):
         copies = halo_copies(phase)
-        for d in range(2):
-            row = 0 if d == 0 else last
-            for e in range(2):
-                es[phase, 2 * d + e] = field[row:row + 1, tile(0 if e == 0 else nt - 1)]
+
+        def send(local, first):
+            for t, value in local.items():
+                field[:, tile(t)] = value
+            for d in range(2):
+                row = 0 if d == 0 else last
+                for t, value in local.items():
+                    xs[phase, d, t:t + 1, :] = value[row:row + 1]
+                if first:
+                    for e in range(2):
+                        es[phase, 2 * d + e] = local[0 if e == 0 else nt - 1][row:row + 1]
+            if not first:
+                return
+            start_all(copies[:12])
+            for d in range(2):
+                packed = None
+                for i in range(ni):
+                    block = local[0 if d == 0 else nt - 1][SUB * i:SUB * (i + 1)]
+                    part = jnp.where(low8 if d == 0 else high8, block, 0.0)
+                    shift = (count * i + d * count) % LANES
+                    part = part if shift == 0 else pltpu.roll(part, shift, 1)
+                    packed = part if packed is None else packed + part
+                ys[phase, d] = packed
+
+        def rest():
+            start_all(copies[12:24])
+            packed = None
             for t in range(nt):
-                xs[phase, d, t:t + 1, :] = field[row:row + 1, tile(t)]
-            packed = None
-            for i in range(ni):
-                block = field[SUB * i:SUB * (i + 1), tile(0 if d == 0 else nt - 1)]
-                part = jnp.where(low8 if d == 0 else high8, block, 0.0)
-                shift = (count * i + d * count) % LANES
-                part = part if shift == 0 else pltpu.roll(part, shift, 1)
+                part = jnp.where(face_c, field[:, tile(t)], 0.0)
+                part = part if t == 0 else pltpu.roll(part, 2 * t, 1)
                 packed = part if packed is None else packed + part
-            ys[phase, d] = packed
-        packed = None
-        for t in range(nt):
-            part = jnp.where(face_c, field[:, tile(t)], 0.0)
-            part = part if t == 0 else pltpu.roll(part, 2 * t, 1)
-            packed = part if packed is None else packed + part
-        zs[phase] = packed
-        start_all(copies)
+            zs[phase] = packed
+            start_all(copies[24:])
+
+        return send, rest
 
     def fold(ref, phase, base, shift=0):
         low = ref[phase, base + 1]
@@ -267,9 +302,10 @@
         out = turn(ref[phase, base], shift) + jnp.where(c == 0, turn(low, shift - last), 0.0)
         return out + jnp.where(c == last, turn(ref[phase, base + 2], shift + last), 0.0)
 
-    def add_halo(phase):
+    def arrive(phase, chosen):
         copies = halo_copies(phase)
-        for index, (copy, _, direction, dst, slot) in enumerate(copies):
+        for index in chosen:
+            _, _, direction, into = copies[index]
             mirror = None
             for d, step in enumerate(direction):
                 if step is not None:
@@ -277,28 +313,54 @@
 
             @pl.when(mirror)
             def _():
-                into = dst.at[phase, slot]
                 pltpu.make_async_copy(into, into, hrecv.at[phase, index]).wait()
+
+    def add_faces(phase):
+        arrive(phase, range(24, 26))
         merged = jnp.where(even, pltpu.roll(zr[phase, 0], LANES - last, 1), pltpu.roll(zr[phase, 1], last, 1))
         for t in range(nt):
             part = merged if t == 0 else pltpu.roll(merged, LANES - 2 * t, 1)
             field[:, tile(t)] += jnp.where(face_c, part, 0.0)
+        arrive(phase, range(18, 24))
         for d in range(2):
             received = fold(yr, phase, 3 * d)
             for i in range(ni):
                 shift = (-count * i - d * count) % LANES
                 part = received if shift == 0 else pltpu.roll(received, shift, 1)
                 field[SUB * i:SUB * (i + 1), tile(0 if d == 0 else nt - 1)] += jnp.where(low8 if d == 0 else high8, part, 0.0)
+        arrive(phase, range(12, 18))
         for d in range(2):
             row = 0 if d == 0 else last
             received = fold(xr, phase, 3 * d)
             for t in range(nt):
-                line = received[t:t + 1]
-                if t == 0:
-                    line += jnp.where(lane1 < count, fold(er, phase, 6 * d, count), 0.0)
-                if t == nt - 1:
-                    line += jnp.where(lane1 >= LANES - count, fold(er, phase, 6 * d + 3, LANES - count), 0.0)
-                field[row:row + 1, tile(t)] += line
+                field[row:row + 1, tile(t)] += received[t:t + 1]
+
+    def take_edges(phase, factor):
+        arrive(phase, range(12))
+        c = lane8 & (count - 1)
+        out = er[phase, 0] + jnp.where(c == 0, pltpu.roll(er[phase, 1], LANES - last, 1), 0.0)
+        out = out + jnp.where(c == last, pltpu.roll(er[phase, 2], last, 1), 0.0)
+        side = (iota((SUB, LANES), 0) & 1) == 0
+        out = jnp.where((side & high8) | (~side & low8), out, 0.0)
+        return out if factor is None else out * factor
+
+    def lines_of(edges):
+        twice = edges + pltpu.roll(edges, SUB // 2, 0)
+        twice = jnp.concatenate([twice, jnp.zeros_like(twice)], axis=0)
+        hi, lo = split(twice)
+        z = mul(jnp.concatenate([hi, lo, hi], axis=1), mzt[...])[:SUB]
+        out = []
+        for t in range(nt):
+            line = ya[:, tile(t)] * z[:, :LANES] + yb[:, tile(t)] * z[:, LANES:]
+            hi = line.astype(BF16).astype(F32)
+            out.append(jnp.concatenate([hi, hi, line - hi, jnp.zeros_like(hi)], axis=0).astype(BF16))
+        return out
+
+    def add_edges(k, edges):
+        for d in range(2):
+            row = 0 if d == 0 else last
+            ws[k, row:row + 1, tile(0)] += pltpu.roll(edges[2 * d:2 * d + 1], count, 1)
+            ws[k, row:row + 1, tile(nt - 1)] += pltpu.roll(edges[2 * d + 1:2 * d + 2], LANES - count, 1)
 
     def send_dots(phase, products):
         packed = None
@@ -327,14 +389,17 @@
         return jnp.sum(jnp.where(diag, line, 0.0), axis=1, keepdims=True)
 
     pl.semaphore_wait(barrier, around_me)
-    send_halo(0)
+    send, rest = send_halo(0)
+    value = field[...]
+    send({t: value[:, tile(t)] for t in range(nt)}, True)
+    rest()
     load_st.wait()
-    build_matrices(st, mx, my, mz)
+    build_matrices(st, mx, my, mz, mzt, ya, yb)
     for r in range(rounds):
         call(r)
         if r < rounds - 1:
             pl.semaphore_wait(ready.at[r], around_me)
-    add_halo(0)
+    add_faces(0)
     ws[0] = field[...]
     gram, rho = {}, [None]
 
@@ -345,19 +410,29 @@
         if k < ITERS:
             rho.append(sums[k + 1:k + 2] / sums[k:k + 1])
 
+    factor = None
     for k in range(ITERS):
-        vector = ws[k]
-        local = apply_patch(vector, mx[...], my[...], mz[...])
-        field[...] = local
-        send_halo(k + 1)
+        edges = []
+
+        def late():
+            edges.append(take_edges(k, factor))
+            return lines_of(edges[0])
+
+        send, rest = send_halo(k + 1)
+        apply_patch(ws[k], mx[...], my[...], mz[...], late, send)
+        rest()
         if k == 0 and rounds > 0:
             pl.semaphore_wait(ready.at[rounds - 1], around_me)
+        add_edges(k, edges[0])
+        vector = ws[k]
         weighted = wt[...] * vector
-        send_dots(k, [weighted * ws[i] for i in range(k + 1)] + [local * vector])
+        send_dots(k, [weighted * ws[i] for i in range(k + 1)] + [field[...] * vector])
         if k > 0:
             gather(k - 1)
-        add_halo(k + 1)
-        ws[k + 1] = field[...] if k == 0 else field[...] * (1.0 / rho[k]) - vector
+            factor = 1.0 / rho[k]
+        add_faces(k + 1)
+        ws[k + 1] = field[...] if k == 0 else field[...] * factor - vector
+    add_edges(ITERS, take_edges(ITERS, factor))
     weighted = wt[...] * ws[ITERS]
     send_dots(ITERS, [weighted * ws[i] for i in range(ITERS + 1)])
     gather(ITERS - 1)
@@ -437,9 +512,12 @@
         in_specs=[pl.BlockSpec(memory_space=pltpu.HBM)] * 2,
         out_specs=(vmem, vmem),
         scratch_shapes=[
-            pltpu.VMEM((count, 6 * count), BF16),
+            pltpu.VMEM((count, 7 * count), BF16),
             pltpu.VMEM((4 * count, 6 * count), BF16),
             pltpu.VMEM((3 * LANES, 2 * LANES), BF16),
+            pltpu.VMEM((3 * LANES, 2 * LANES), BF16),
+            pltpu.VMEM((SUB, area), F32),
+            pltpu.VMEM((SUB, area), F32),
             pltpu.VMEM((count, area), F32),
             pltpu.VMEM((count, area), F32),
             pltpu.VMEM((halos, count, LANES), F32),
@@ -449,7 +527,7 @@
             pltpu.VMEM((halos, 2, SUB, LANES), F32),
             pltpu.VMEM((halos, 6, SUB, LANES), F32),
             pltpu.VMEM((halos, 4, 1, LANES), F32),
-            pltpu.VMEM((halos, 12, 1, LANES), F32),
+            pltpu.VMEM((halos, 3, SUB, LANES), F32),
             pltpu.VMEM((halos, total, 1, LANES), F32),
             pltpu.SemaphoreType.DMA((halos, 26)),
             pltpu.SemaphoreType.DMA((halos, 26)),

time: 41.6 us -> 40.1 us (0.964)
  Pallas kernels: 40.8 us -> 39.3 us
    pallas_call x1, Pallas kernels: 39.9 us -> 38.5 us  [shards(): call(*(pltpu.with_memory_space_constraint(x, pltpu.HBM) for x in (start[0...]
where the time goes in v3:
time: 40.1 us; the launch traced here: 40 us
  Pallas kernels  39.3 us (98%)
  between operations  0.64 us (2%)
    pallas_call x1, Pallas kernels, shards(): call(*(pltpu.with_memory_space_constraint(x, pltpu.HBM) for x in (start[0...  38.5 us
    pallas_call x1, Pallas kernels, shards(): put(*call(*(pltpu.with_memory_space_constraint(x, pltpu.HBM) for x in (st...  0.88 us

profile of v3, /device:TPU:0, one launch (start us, length us, event | category | flops | bytes accessed | tf_op | source)
XLA Modules:
  0.0 40.0 jit_solution(11274281426650316421)
XLA Ops:
  0.6 38.5 %shard_map.41 = (f32[5,32,1024]{2,1,0:T(8,128)S(1)}, f32[1,2,5]{2,1,0:T(2,128)S(1)}) custom-call(f32[32,1024]{1,0:T(8,128)} %bitcast.3, f32[6,32,32]{2,1,0:T(8,128)} %bitcast.4), custom_call_target="tpu_custom_call" | custom-call | tf_op jit(solution)/shard_map/pallas_call | solution.py:553
  39.1 0.9 %shard_map.42 = (f32[5,32,1024]{2,1,0:T(8,128)}, f32[1,2,5]{2,1,0:T(2,128)}) custom-call(f32[5,32,1024]{2,1,0:T(8,128)S(1)} %get-tuple-element.6.basis, f32[1,2,5]{2,1,0:T(2,128)S(1)} %get-tuple-element.7.coef), custom_call_target="tpu_custom_call" | custom-call | tf_op jit(solution)/shard_map/pallas_call | solution.py:553

commit v4 on v3

--- a/solution.py
+++ b/solution.py
@@ -11,6 +11,7 @@
 LANES = 128
 SUB = 8
 MESH = pl.DeviceIdType.MESH
+KINDS = ("e", "x", "y", "z")
 F32 = jnp.float32
 BF16 = jnp.bfloat16
 HIGHEST = lax.Precision.HIGHEST
@@ -89,49 +90,36 @@
     yb[...] = jnp.where(upper, mass, 0.0)
 
 
-def apply_patch(u, mx, my, mz, late, send):
-    count, area = u.shape
-    ni, nt = count // SUB, area // LANES
-    rows = nt * SUB
-    terms = []
-    for h in range(2):
-        group = range(h * ni // 2, (h + 1) * ni // 2)
-        tiles = jnp.concatenate([u[SUB * i:SUB * (i + 1), LANES * t:LANES * (t + 1)] for i in group for t in range(nt)], axis=0)
-        tiles = swap(tiles.reshape(-1, SUB, LANES)).reshape(-1, LANES)
-        hi, lo = split(tiles)
-        z = mul(jnp.concatenate([hi, lo, hi], axis=1), mz)
-        packed = []
-        for slot in range(2):
-            part = z[:, slot * LANES:(slot + 1) * LANES]
-            wide = jnp.concatenate([part[rows * i:rows * (i + 1)] for i in range(len(group))], axis=1)
-            hi, lo = split(wide)
-            packed.append(jnp.concatenate([hi, hi, lo], axis=0))
-        both = mul(my, packed[0])
-        terms.append((both[:rows], both[rows:] + mul(my[:rows], packed[1])))
-    lines = late()
-    half = ni // 2
-    order = [0, nt - 1] + list(range(1, nt - 1))
-    for at in range(0, nt, 2):
-        pair = order[at:at + 2]
-        stacked = jnp.stack([
-            terms[i // half][k][SUB * t:SUB * (t + 1), LANES * (i % half):LANES * (i % half + 1)]
-            for k in range(2) for t in pair for i in range(ni)
-        ])
-        stacked = swap(stacked)
-        pieces = []
-        for k in range(2):
-            back = jnp.concatenate([
-                jnp.concatenate([stacked[(k * 2 + n) * ni + i] for i in range(ni)], axis=0) for n in range(2)
-            ], axis=1)
-            hi, lo = split(back)
-            pieces += [hi, hi, lo]
-        pieces.append(jnp.concatenate([lines[t] for t in pair], axis=1))
-        out = mul(mx, jnp.concatenate(pieces, axis=0))
-        send({t: out[:, LANES * n:LANES * (n + 1)] for n, t in enumerate(pair)}, at == 0)
+def through_z(u, rows_of, mz):
+    nt = u(rows_of[0]).shape[1] // LANES
+    blocks = [u(i) for i in rows_of]
+    tiles = jnp.concatenate([block[:, LANES * t:LANES * (t + 1)] for block in blocks for t in range(nt)], axis=0)
+    tiles = swap(tiles.reshape(-1, SUB, LANES)).reshape(-1, LANES)
+    hi, lo = split(tiles)
+    return mul(jnp.concatenate([hi, lo, hi], axis=1), mz)
+
+
+def through_y(z, my):
+    rows = my.shape[0] // 2
+    packed = []
+    for slot in range(2):
+        part = z[:, slot * LANES:(slot + 1) * LANES]
+        wide = jnp.concatenate([part[at:at + rows] for at in range(0, part.shape[0], rows)], axis=1)
+        hi, lo = split(wide)
+        packed.append(jnp.concatenate([hi, hi, lo], axis=0))
+    both = mul(my, packed[0])
+    return both[:rows], both[rows:] + mul(my[:rows], packed[1])
+
+
+def swap_back(terms, t):
+    width = terms[0].shape[1] // LANES
+    stacked = jnp.stack([term[SUB * t:SUB * (t + 1), LANES * n:LANES * (n + 1)] for term in terms for n in range(width)])
+    stacked = swap(stacked)
+    return [[stacked[k * width + n] for n in range(width)] for k in range(2)]
 
 
 def kernel(sizes, start_in, st_in, basis, coef, mx, my, mz, mzt, ya, yb, wt, field,
-           zs, zr, xs, xr, ys, yr, es, er, rows, hsend, hrecv, rsend, rrecv, ready, ws, start, st, loads):
+           zs, zr, xs, xz, xr, ys, yz, yr, es, ez, er, edge_slots, rows, hsend, hrecv, rsend, rrecv, ready, ws, start, st, loads):
     load_start = pltpu.make_async_copy(start_in, start, loads.at[0])
     load_st = pltpu.make_async_copy(st_in, st, loads.at[1])
     load_start.start()
@@ -186,10 +174,16 @@
                         def _():
                             act(target)
 
-    around_me = 1
-    for d in range(3):
-        around_me = around_me * (1 + (coords[d] > 0).astype(jnp.int32) + (coords[d] < sizes[d] - 1).astype(jnp.int32))
-    around_me = around_me - 1
+    beside = [(coords[d] > 0).astype(jnp.int32) + (coords[d] < sizes[d] - 1).astype(jnp.int32) for d in range(3)]
+    around_me = (1 + beside[0]) * (1 + beside[1]) * (1 + beside[2]) - 1
+    amounts = {
+        "e": lambda x, y, z: x * y * (1 + z),
+        "x": lambda x, y, z: x * (1 + z),
+        "y": lambda x, y, z: y * (1 + z),
+        "z": lambda x, y, z: z,
+    }
+    sides = [(0,) if size == 1 else (1,) if size == 2 else (1, 2) for size in sizes]
+    slots = {"e": edge_slots, "x": xr, "y": yr, "z": zr}
 
     rounds = max(sizes) - 2
 
@@ -221,34 +215,34 @@
         return slice(t * LANES, (t + 1) * LANES)
 
     def halo_copies(phase):
-        out = []
-
-        def add(src, into, *direction):
+        out = {name: [] for name in ("e", "ez", "x", "xz", "y", "yz", "z")}
+
+        def add(name, src, into, *direction):
             there_all, target = None, {}
             for d, step in enumerate(direction):
                 if step is not None:
                     there_all = there[d][step] if there_all is None else there_all & there[d][step]
             target = tuple(c if step is None else c + 2 * step - 1 for c, step in zip(coords, direction))
             copy = pltpu.make_async_remote_copy(
-                src_ref=src, dst_ref=into, send_sem=hsend.at[phase, len(out)],
-                recv_sem=hrecv.at[phase, len(out)], device_id=target, device_id_type=MESH)
-            out.append((copy, there_all, direction, into))
+                src_ref=src, dst_ref=into, send_sem=hsend.at[KINDS.index(name[0])],
+                recv_sem=hrecv.at[phase % 2, KINDS.index(name[0])], device_id=target, device_id_type=MESH)
+            out[name].append((copy, there_all))
 
         for z in (None, 1, 0):
+            back, kind = (0, "") if z is None else (2 - z, "z")
             for d in range(2):
                 for e in range(2):
-                    back = 0 if z is None else 2 - z
-                    add(es.at[phase, 2 * d + e], er.at[phase, back, pl.ds(2 * (1 - d) + 1 - e, 1)], d, e, z)
-        for z in (None, 1, 0):
-            back = 0 if z is None else 2 - z
+                    q = pl.ds(2 * d + e, 1)
+                    src = es.at[phase, q] if z is None else ez.at[phase, z, q]
+                    add("e" + kind, src, er.at[phase, back, pl.ds(2 * (1 - d) + 1 - e, 1)], d, e, z)
             for d in range(2):
-                add(xs.at[phase, d], xr.at[phase, (1 - d) * 3 + back], d, None, z)
-        for z in (None, 1, 0):
-            back = 0 if z is None else 2 - z
+                src = xs.at[phase, d] if z is None else xz.at[phase, z, d]
+                add("x" + kind, src, xr.at[6 * phase + (1 - d) * 3 + back], d, None, z)
             for d in range(2):
-                add(ys.at[phase, d], yr.at[phase, (1 - d) * 3 + back], None, d, z)
+                src = ys.at[phase, d] if z is None else yz.at[phase, z, d]
+                add("y" + kind, src, yr.at[6 * phase + (1 - d) * 3 + back], None, d, z)
         for d in range(2):
-            add(zs.at[phase], zr.at[phase, 1 - d], None, None, d)
+            add("z", zs.at[phase], zr.at[2 * phase + 1 - d], None, None, d)
         return out
 
     def start_all(copies):
@@ -256,6 +250,12 @@
             @pl.when(exists)
             def _():
                 copy.start()
+
+    def across(value, z):
+        c = iota(value.shape, 1) & (count - 1)
+        if z == 1:
+            return jnp.where(c == 0, pltpu.roll(value, LANES - last, 1), 0.0)
+        return jnp.where(c == last, pltpu.roll(value, last, 1), 0.0)
 
     def send_halo(phase):
         copies = halo_copies(phase)
@@ -269,77 +269,83 @@
                     xs[phase, d, t:t + 1, :] = value[row:row + 1]
                 if first:
                     for e in range(2):
-                        es[phase, 2 * d + e] = local[0 if e == 0 else nt - 1][row:row + 1]
-            if not first:
-                return
-            start_all(copies[:12])
-            for d in range(2):
-                packed = None
-                for i in range(ni):
-                    block = local[0 if d == 0 else nt - 1][SUB * i:SUB * (i + 1)]
-                    part = jnp.where(low8 if d == 0 else high8, block, 0.0)
-                    shift = (count * i + d * count) % LANES
-                    part = part if shift == 0 else pltpu.roll(part, shift, 1)
-                    packed = part if packed is None else packed + part
-                ys[phase, d] = packed
+                        es[phase, 2 * d + e:2 * d + e + 1, :] = local[0 if e == 0 else nt - 1][row:row + 1]
+            if first:
+                start_all(copies["e"])
+                for d in range(2):
+                    packed = None
+                    for i in range(ni):
+                        block = local[0 if d == 0 else nt - 1][SUB * i:SUB * (i + 1)]
+                        part = jnp.where(low8 if d == 0 else high8, block, 0.0)
+                        shift = (count * i + d * count) % LANES
+                        part = part if shift == 0 else pltpu.roll(part, shift, 1)
+                        packed = part if packed is None else packed + part
+                    ys[phase, d] = packed
 
         def rest():
-            start_all(copies[12:24])
+            start_all(copies["x"])
+            start_all(copies["y"])
+            for z in range(2):
+                ez[phase, z] = across(es[phase], z)
+            start_all(copies["ez"])
+            for z in range(2):
+                for d in range(2):
+                    xz[phase, z, d] = across(xs[phase, d], z)
+            start_all(copies["xz"])
+            for z in range(2):
+                for d in range(2):
+                    yz[phase, z, d] = across(ys[phase, d], z)
+            start_all(copies["yz"])
             packed = None
             for t in range(nt):
                 part = jnp.where(face_c, field[:, tile(t)], 0.0)
                 part = part if t == 0 else pltpu.roll(part, 2 * t, 1)
                 packed = part if packed is None else packed + part
             zs[phase] = packed
-            start_all(copies[24:])
+            start_all(copies["z"])
 
         return send, rest
 
-    def fold(ref, phase, base, shift=0):
-        low = ref[phase, base + 1]
-        c = iota(low.shape, 1) & (count - 1)
-        turn = lambda x, by: x if by % LANES == 0 else pltpu.roll(x, by % LANES, 1)
-        out = turn(ref[phase, base], shift) + jnp.where(c == 0, turn(low, shift - last), 0.0)
-        return out + jnp.where(c == last, turn(ref[phase, base + 2], shift + last), 0.0)
-
-    def arrive(phase, chosen):
-        copies = halo_copies(phase)
-        for index in chosen:
-            _, _, direction, into = copies[index]
-            mirror = None
-            for d, step in enumerate(direction):
-                if step is not None:
-                    mirror = there[d][1 - step] if mirror is None else mirror & there[d][1 - step]
-
-            @pl.when(mirror)
-            def _():
-                pltpu.make_async_copy(into, into, hrecv.at[phase, index]).wait()
-
-    def add_faces(phase):
-        arrive(phase, range(24, 26))
-        merged = jnp.where(even, pltpu.roll(zr[phase, 0], LANES - last, 1), pltpu.roll(zr[phase, 1], last, 1))
+    def take(kind, sem, phases):
+        mine = amounts[kind](*beside)
+        for amount in sorted({amounts[kind](x, y, z) for x in sides[0] for y in sides[1] for z in sides[2]}):
+            if amount:
+                @pl.when(mine == amount)
+                def _():
+                    into = slots[kind].at[pl.ds(0, amount * phases)]
+                    pltpu.make_async_copy(into, into, sem).wait()
+
+    def arrive(phase, kind):
+        take(kind, hrecv.at[phase % 2, KINDS.index(kind)], 1)
+
+    def sent(kind):
+        take(kind, hsend.at[KINDS.index(kind)], ITERS + 1)
+
+    def add_yz(phase):
+        arrive(phase, "z")
+        merged = jnp.where(even, pltpu.roll(zr[2 * phase], LANES - last, 1), pltpu.roll(zr[2 * phase + 1], last, 1))
         for t in range(nt):
             part = merged if t == 0 else pltpu.roll(merged, LANES - 2 * t, 1)
             field[:, tile(t)] += jnp.where(face_c, part, 0.0)
-        arrive(phase, range(18, 24))
+        arrive(phase, "y")
         for d in range(2):
-            received = fold(yr, phase, 3 * d)
+            received = yr[6 * phase + 3 * d] + yr[6 * phase + 3 * d + 1] + yr[6 * phase + 3 * d + 2]
             for i in range(ni):
                 shift = (-count * i - d * count) % LANES
                 part = received if shift == 0 else pltpu.roll(received, shift, 1)
                 field[SUB * i:SUB * (i + 1), tile(0 if d == 0 else nt - 1)] += jnp.where(low8 if d == 0 else high8, part, 0.0)
-        arrive(phase, range(12, 18))
+
+    def add_x(phase):
+        arrive(phase, "x")
         for d in range(2):
             row = 0 if d == 0 else last
-            received = fold(xr, phase, 3 * d)
+            received = xr[6 * phase + 3 * d] + xr[6 * phase + 3 * d + 1] + xr[6 * phase + 3 * d + 2]
             for t in range(nt):
                 field[row:row + 1, tile(t)] += received[t:t + 1]
 
     def take_edges(phase, factor):
-        arrive(phase, range(12))
-        c = lane8 & (count - 1)
-        out = er[phase, 0] + jnp.where(c == 0, pltpu.roll(er[phase, 1], LANES - last, 1), 0.0)
-        out = out + jnp.where(c == last, pltpu.roll(er[phase, 2], last, 1), 0.0)
+        arrive(phase, "e")
+        out = er[phase, 0] + er[phase, 1] + er[phase, 2]
         side = (iota((SUB, LANES), 0) & 1) == 0
         out = jnp.where((side & high8) | (~side & low8), out, 0.0)
         return out if factor is None else out * factor
@@ -399,8 +405,6 @@
         call(r)
         if r < rounds - 1:
             pl.semaphore_wait(ready.at[r], around_me)
-    add_faces(0)
-    ws[0] = field[...]
     gram, rho = {}, [None]
 
     def gather(k):
@@ -411,27 +415,55 @@
             rho.append(sums[k + 1:k + 2] / sums[k:k + 1])
 
     factor = None
+
+    def advance(k, inner):
+        for i in range(ni):
+            if (0 < i < ni - 1) == inner:
+                part = slice(SUB * i, SUB * (i + 1))
+                ws[k, part] = field[part] if k < 2 else field[part] * factor - ws[k - 1, part]
+
+    middle, ends = list(range(1, ni - 1)), [0, ni - 1]
+    block = lambda k: lambda i: ws[k, SUB * i:SUB * (i + 1)]
     for k in range(ITERS):
-        edges = []
-
-        def late():
-            edges.append(take_edges(k, factor))
-            return lines_of(edges[0])
-
+        add_yz(k)
+        advance(k, True)
+        inner = through_z(block(k), middle, mz[...])
+        add_x(k)
+        advance(k, False)
+        outer = through_z(block(k), ends, mz[...])
+        inner = through_y(inner, my[...])
+        edges = take_edges(k, factor)
+        lines = lines_of(edges)
+        outer = through_y(outer, my[...])
         send, rest = send_halo(k + 1)
-        apply_patch(ws[k], mx[...], my[...], mz[...], late, send)
+        order = [0, nt - 1] + list(range(1, nt - 1))
+        for at in range(0, nt, 2):
+            pieces = [[], []]
+            for t in order[at:at + 2]:
+                mid, end = swap_back(inner, t), swap_back(outer, t)
+                for n in range(2):
+                    pieces[n].append(jnp.concatenate([end[n][0]] + mid[n] + [end[n][1]], axis=0))
+            stack = []
+            for n in range(2):
+                hi, lo = split(jnp.concatenate(pieces[n], axis=1))
+                stack += [hi, hi, lo]
+            stack.append(jnp.concatenate([lines[t] for t in order[at:at + 2]], axis=1))
+            out = mul(mx[...], jnp.concatenate(stack, axis=0))
+            send({t: out[:, LANES * n:LANES * (n + 1)] for n, t in enumerate(order[at:at + 2])}, at == 0)
         rest()
         if k == 0 and rounds > 0:
             pl.semaphore_wait(ready.at[rounds - 1], around_me)
-        add_edges(k, edges[0])
+        add_edges(k, edges)
         vector = ws[k]
         weighted = wt[...] * vector
         send_dots(k, [weighted * ws[i] for i in range(k + 1)] + [field[...] * vector])
         if k > 0:
             gather(k - 1)
             factor = 1.0 / rho[k]
-        add_faces(k + 1)
-        ws[k + 1] = field[...] if k == 0 else field[...] * factor - vector
+    add_yz(ITERS)
+    advance(ITERS, True)
+    add_x(ITERS)
+    advance(ITERS, False)
     add_edges(ITERS, take_edges(ITERS, factor))
     weighted = wt[...] * ws[ITERS]
     send_dots(ITERS, [weighted * ws[i] for i in range(ITERS + 1)])
@@ -465,6 +497,11 @@
 
     for k in range(ITERS):
         column(k)
+    for kind in KINDS:
+        sent(kind)
+    for phase in range(ITERS):
+        others = rows.at[phase, pl.ds(0, total - 1)]
+        pltpu.make_async_copy(others, others, rsend.at[phase]).wait()
     gather(ITERS)
     column(ITERS)
     row2, col2 = iota(coef.shape[1:], 0), iota(coef.shape[1:], 1)
@@ -480,14 +517,8 @@
         coefs = jnp.where((row2 == 1) & (col2 == k), beta, coefs)
     coef[0] = coefs
 
-    for phase in range(ITERS + 1):
-        for copy, exists, *_ in halo_copies(phase):
-            @pl.when(exists)
-            def _():
-                copy.wait_send()
-    for phase in range(ITERS + 1):
-        others = rows.at[phase, pl.ds(0, total - 1)]
-        pltpu.make_async_copy(others, others, rsend.at[phase]).wait()
+    others = rows.at[ITERS, pl.ds(0, total - 1)]
+    pltpu.make_async_copy(others, others, rsend.at[ITERS]).wait()
 
 
 def store(basis, coef, basis_out, coef_out, sems):
@@ -521,16 +552,20 @@
             pltpu.VMEM((count, area), F32),
             pltpu.VMEM((count, area), F32),
             pltpu.VMEM((halos, count, LANES), F32),
-            pltpu.VMEM((halos, 2, count, LANES), F32),
+            pltpu.VMEM((halos * 2, count, LANES), F32),
             pltpu.VMEM((halos, 2, nt, LANES), F32),
-            pltpu.VMEM((halos, 6, nt, LANES), F32),
+            pltpu.VMEM((halos, 2, 2, nt, LANES), F32),
+            pltpu.VMEM((halos * 6, nt, LANES), F32),
             pltpu.VMEM((halos, 2, SUB, LANES), F32),
-            pltpu.VMEM((halos, 6, SUB, LANES), F32),
-            pltpu.VMEM((halos, 4, 1, LANES), F32),
+            pltpu.VMEM((halos, 2, 2, SUB, LANES), F32),
+            pltpu.VMEM((halos * 6, SUB, LANES), F32),
+            pltpu.VMEM((halos, 4, LANES), F32),
+            pltpu.VMEM((halos, 2, 4, LANES), F32),
             pltpu.VMEM((halos, 3, SUB, LANES), F32),
+            pltpu.VMEM((halos * 12, 1, LANES), F32),
             pltpu.VMEM((halos, total, 1, LANES), F32),
-            pltpu.SemaphoreType.DMA((halos, 26)),
-            pltpu.SemaphoreType.DMA((halos, 26)),
+            pltpu.SemaphoreType.DMA((len(KINDS),)),
+            pltpu.SemaphoreType.DMA((2, len(KINDS))),
             pltpu.SemaphoreType.DMA((halos,)),
             pltpu.SemaphoreType.DMA((halos,)),
             pltpu.SemaphoreType.REGULAR((max(1, max(sizes) - 2),)),

time: 40.1 us -> 36.5 us (0.910)
  Pallas kernels: 39.3 us -> 35.7 us
    pallas_call x1, Pallas kernels: 38.5 us -> 34.8 us  [shards(): call(*(pltpu.with_memory_space_constraint(x, pltpu.HBM) for x in (start[0...]
where the time goes in v4:
time: 36.5 us; the launch traced here: 36.3 us
  Pallas kernels  35.7 us (98%)
  between operations  0.64 us (2%)
    pallas_call x1, Pallas kernels, shards(): call(*(pltpu.with_memory_space_constraint(x, pltpu.HBM) for x in (start[0...  34.8 us
    pallas_call x1, Pallas kernels, shards(): put(*call(*(pltpu.with_memory_space_constraint(x, pltpu.HBM) for x in (st...  0.88 us

profile of v4, /device:TPU:0, one launch (start us, length us, event | category | flops | bytes accessed | tf_op | source)
XLA Modules:
  0.0 36.3 jit_solution(3852292716822191680)
XLA Ops:
  0.6 34.8 %shard_map.41 = (f32[5,32,1024]{2,1,0:T(8,128)S(1)}, f32[1,2,5]{2,1,0:T(2,128)S(1)}) custom-call(f32[32,1024]{1,0:T(8,128)} %bitcast.3, f32[6,32,32]{2,1,0:T(8,128)} %bitcast.4), custom_call_target="tpu_custom_call" | custom-call | tf_op jit(solution)/shard_map/pallas_call | solution.py:588
  35.4 0.9 %shard_map.42 = (f32[5,32,1024]{2,1,0:T(8,128)}, f32[1,2,5]{2,1,0:T(2,128)}) custom-call(f32[5,32,1024]{2,1,0:T(8,128)S(1)} %get-tuple-element.6.basis, f32[1,2,5]{2,1,0:T(2,128)S(1)} %get-tuple-element.7.coef), custom_call_target="tpu_custom_call" | custom-call | tf_op jit(solution)/shard_map/pallas_call | solution.py:588

commit v5 on v4

--- a/solution.py
+++ b/solution.py
@@ -45,7 +45,7 @@
     return out
 
 
-def build_matrices(st, mx, my, mz, mzt, ya, yb):
+def build_matrices(st, mx, my, ym, mz, mzt, ya, yb):
     count = st.shape[1]
     wide = LANES
     spread = ((iota((wide, count), 0) & (count - 1)) == iota((wide, count), 1)).astype(F32)
@@ -60,7 +60,9 @@
             ref[2 * wide:3 * wide, slot * wide:(slot + 1) * wide] = lo
     rows = 2 * count
     r = iota((rows, count), 0)
-    pick = (((r >> 3) * 4 + (r & 3)) == iota((rows, count), 1)).astype(F32)
+    place = r >> 3
+    place = jnp.where(place == 0, 0, jnp.where(place == 1, rows // SUB - 1, place - 1))
+    pick = ((place * 4 + (r & 3)) == iota((rows, count), 1)).astype(F32)
     cols = 3 * rows
     l = iota((count, cols), 1) & (rows - 1)
     pick_t = (((l >> 3) * 4 + (l & 3)) == iota((count, cols), 0)).astype(F32)
@@ -69,11 +71,19 @@
     for slot, which in ((0, 4), (1, 1)):
         big = jnp.where(same, exact(exact(pick, st[which]), pick_t), 0.0)
         hi = big.astype(BF16).astype(F32)
-        my[slot * rows:(slot + 1) * rows, :] = jnp.where(middle, big - hi, hi).astype(BF16)
+        big = jnp.where(middle, big - hi, hi).astype(BF16)
+        if slot == 0:
+            ym[...] = big
+        for at in range(0, rows, 2 * SUB):
+            my[2 * at + 2 * SUB * slot:2 * at + 2 * SUB * (slot + 1), :] = big[at:at + 2 * SUB]
     cols = 7 * count
     row, col = iota((count, cols), 0), iota((count, cols), 1)
-    block, extra, part = col >> 5, col >= 6 * count, (col >> 3) & 3
-    source = jnp.where(extra, jnp.where((col & 2) == 0, 0, count - 1), col & (count - 1))
+    extra, part = col >= 6 * count, (col >> 3) & 3
+    wide, within = 2 * SUB, col & (2 * SUB - 1)
+    outer = (col >= 6 * wide) & ~extra
+    block = jnp.where(outer, (col >> 4) - 6, col >> 4)
+    source = jnp.where(outer, jnp.where(within < SUB, within, count - wide + within), SUB + within)
+    source = jnp.where(extra, jnp.where((col & 2) == 0, 0, count - 1), source)
     tile = (source == row).astype(F32)
     big = jnp.where((extra & ((col & 4) == 0)) | (~extra & (block >= 3)), exact(st[3], tile), exact(st[0], tile))
     hi = big.astype(BF16).astype(F32)
@@ -99,31 +109,31 @@
     return mul(jnp.concatenate([hi, lo, hi], axis=1), mz)
 
 
-def through_y(z, my):
-    rows = my.shape[0] // 2
+def through_y(z, my, ym):
+    rows = ym.shape[0]
     packed = []
     for slot in range(2):
         part = z[:, slot * LANES:(slot + 1) * LANES]
         wide = jnp.concatenate([part[at:at + rows] for at in range(0, part.shape[0], rows)], axis=1)
         hi, lo = split(wide)
         packed.append(jnp.concatenate([hi, hi, lo], axis=0))
+    second = mul(ym, packed[1])
     both = mul(my, packed[0])
-    return both[:rows], both[rows:] + mul(my[:rows], packed[1])
-
-
-def swap_back(terms, t):
+    pairs = []
+    for at in range(0, rows, 2 * SUB):
+        pairs.append((both[2 * at:2 * at + 2 * SUB], both[2 * at + 2 * SUB:2 * at + 4 * SUB] + second[at:at + 2 * SUB]))
+    return pairs
+
+
+def swap_back(terms, n):
     width = terms[0].shape[1] // LANES
-    stacked = jnp.stack([term[SUB * t:SUB * (t + 1), LANES * n:LANES * (n + 1)] for term in terms for n in range(width)])
+    stacked = jnp.stack([term[SUB * n:SUB * (n + 1), LANES * i:LANES * (i + 1)] for term in terms for i in range(width)])
     stacked = swap(stacked)
-    return [[stacked[k * width + n] for n in range(width)] for k in range(2)]
-
-
-def kernel(sizes, start_in, st_in, basis, coef, mx, my, mz, mzt, ya, yb, wt, field,
-           zs, zr, xs, xz, xr, ys, yz, yr, es, ez, er, edge_slots, rows, hsend, hrecv, rsend, rrecv, ready, ws, start, st, loads):
-    load_start = pltpu.make_async_copy(start_in, start, loads.at[0])
-    load_st = pltpu.make_async_copy(st_in, st, loads.at[1])
-    load_start.start()
-    load_st.start()
+    return [[stacked[k * width + i] for i in range(width)] for k in range(2)]
+
+
+def kernel(sizes, start_in, st_in, basis, coef, mx, my, ym, mz, mzt, ya, yb, wt, field,
+           zs, zr, xs, xz, xr, ys, yz, yr, es, ez, er, edge_slots, rows, hsend, hrecv, rsend, rrecv, ready, ws, start, st, loads, mid):
     nx, ny, nz = sizes
     total = nx * ny * nz
     count, area = start.shape
@@ -135,8 +145,10 @@
     coords = (px, py, pz)
     there = [[coords[d] > 0, coords[d] < sizes[d] - 1] for d in range(3)]
 
-    for ref in (zr, xr, yr, er):
-        ref[...] = jnp.zeros_like(ref)
+    load_start = pltpu.make_async_copy(start_in, start, loads.at[0])
+    load_st = pltpu.make_async_copy(st_in, st, loads.at[1])
+    load_start.start()
+    load_st.start()
     barrier = pltpu.get_barrier_semaphore()
 
     def peer(k):
@@ -151,7 +163,8 @@
 
             lax.fori_loop(1, total, step, 0)
             return
-        around = [[lax.rem(coords[d] + k, sizes[d]) if k else coords[d] for k in range(sizes[d])] for d in range(3)]
+        step = lambda d, k: coords[d] ^ k if sizes[d] & (sizes[d] - 1) == 0 else lax.rem(coords[d] + k, sizes[d])
+        around = [[step(d, k) if k else coords[d] for k in range(sizes[d])] for d in range(3)]
         for ky in range(ny - 1, -1, -1):
             for kx in range(nx - 1, -1, -1):
                 for kz in range(nz):
@@ -159,20 +172,18 @@
                         act((around[0][kx], around[1][ky], around[2][kz]))
 
     def neighbours(act):
-        for dx in (-1, 0, 1):
-            for dy in (-1, 0, 1):
-                for dz in (-1, 0, 1):
-                    if dx or dy or dz:
-                        target = (px + dx, py + dy, pz + dz)
-                        inside = None
-                        for d, step in enumerate((dx, dy, dz)):
-                            if step:
-                                side = there[d][(step + 1) // 2]
-                                inside = side if inside is None else inside & side
-
-                        @pl.when(inside)
-                        def _():
-                            act(target)
+        around = [(dx, dy, dz) for dx in (-1, 0, 1) for dy in (-1, 0, 1) for dz in (0, -1, 1) if dx or dy or dz]
+        for dx, dy, dz in sorted(around, key=lambda step: -2 * abs(step[0]) - abs(step[1])):
+            target = (px + dx, py + dy, pz + dz)
+            inside = None
+            for d, step in enumerate((dx, dy, dz)):
+                if step:
+                    side = there[d][(step + 1) // 2]
+                    inside = side if inside is None else inside & side
+
+            @pl.when(inside)
+            def _():
+                act(target)
 
     beside = [(coords[d] > 0).astype(jnp.int32) + (coords[d] < sizes[d] - 1).astype(jnp.int32) for d in range(3)]
     around_me = (1 + beside[0]) * (1 + beside[1]) * (1 + beside[2]) - 1
@@ -191,6 +202,29 @@
         neighbours(lambda target: pl.semaphore_signal(ready.at[r], inc=1, device_id=target, device_id_type=MESH))
 
     neighbours(lambda target: pl.semaphore_signal(barrier, inc=1, device_id=target, device_id_type=MESH))
+
+    def clear(missing, refs):
+        @pl.when(missing)
+        def _():
+            for ref in refs:
+                ref[...] = jnp.zeros_like(ref)
+
+    phases = range(ITERS + 1)
+    for phase in phases:
+        er[phase, :, SUB // 2:, :] = jnp.zeros((3, SUB // 2, LANES), F32)
+    for d in range(2):
+        clear(~there[2][d], [zr.at[2 * phase + d] for phase in phases])
+        clear(~there[0][d], [xr.at[pl.ds(6 * phase + 3 * d, 3)] for phase in phases])
+        clear(~there[1][d], [yr.at[pl.ds(6 * phase + 3 * d, 3)] for phase in phases])
+        for z in range(2):
+            clear(there[0][d] & ~there[2][z], [xr.at[6 * phase + 3 * d + 1 + z] for phase in phases])
+            clear(there[1][d] & ~there[2][z], [yr.at[6 * phase + 3 * d + 1 + z] for phase in phases])
+        for e in range(2):
+            q = pl.ds(2 * d + e, 1)
+            both = there[0][d] & there[1][e]
+            clear(~both, [er.at[phase, :, q] for phase in phases])
+            for z in range(2):
+                clear(both & ~there[2][z], [er.at[phase, 1 + z, q] for phase in phases])
 
     def shared(index, d):
         return ((index == 0) & there[d][0]) | ((index == last) & there[d][1])
@@ -271,7 +305,6 @@
                     for e in range(2):
                         es[phase, 2 * d + e:2 * d + e + 1, :] = local[0 if e == 0 else nt - 1][row:row + 1]
             if first:
-                start_all(copies["e"])
                 for d in range(2):
                     packed = None
                     for i in range(ni):
@@ -284,6 +317,7 @@
 
         def rest():
             start_all(copies["x"])
+            start_all(copies["e"])
             start_all(copies["y"])
             for z in range(2):
                 ez[phase, z] = across(es[phase], z)
@@ -400,7 +434,7 @@
     send({t: value[:, tile(t)] for t in range(nt)}, True)
     rest()
     load_st.wait()
-    build_matrices(st, mx, my, mz, mzt, ya, yb)
+    build_matrices(st, mx, my, ym, mz, mzt, ya, yb)
     for r in range(rounds):
         call(r)
         if r < rounds - 1:
@@ -431,25 +465,30 @@
         add_x(k)
         advance(k, False)
         outer = through_z(block(k), ends, mz[...])
-        inner = through_y(inner, my[...])
+        inner = through_y(inner, my[...], ym[...])
         edges = take_edges(k, factor)
+        for p in range(nt // 2):
+            swapped = [swap_back(inner[p], n) for n in range(2)]
+            for j in range(2):
+                hi, lo = split(jnp.concatenate([jnp.concatenate(part[j], axis=0) for part in swapped], axis=1))
+                mid[p, 2 * j] = hi
+                mid[p, 2 * j + 1] = lo
+        outer = through_y(outer, my[...], ym[...])
         lines = lines_of(edges)
-        outer = through_y(outer, my[...])
         send, rest = send_halo(k + 1)
         order = [0, nt - 1] + list(range(1, nt - 1))
-        for at in range(0, nt, 2):
-            pieces = [[], []]
-            for t in order[at:at + 2]:
-                mid, end = swap_back(inner, t), swap_back(outer, t)
-                for n in range(2):
-                    pieces[n].append(jnp.concatenate([end[n][0]] + mid[n] + [end[n][1]], axis=0))
+        for p in range(nt // 2):
+            pair = order[2 * p:2 * p + 2]
             stack = []
-            for n in range(2):
-                hi, lo = split(jnp.concatenate(pieces[n], axis=1))
+            for j in range(2):
+                stack += [mid[p, 2 * j], mid[p, 2 * j], mid[p, 2 * j + 1]]
+            swapped = [swap_back(outer[p], n) for n in range(2)]
+            for j in range(2):
+                hi, lo = split(jnp.concatenate([jnp.concatenate(part[j], axis=0) for part in swapped], axis=1))
                 stack += [hi, hi, lo]
-            stack.append(jnp.concatenate([lines[t] for t in order[at:at + 2]], axis=1))
+            stack.append(jnp.concatenate([lines[t] for t in pair], axis=1))
             out = mul(mx[...], jnp.concatenate(stack, axis=0))
-            send({t: out[:, LANES * n:LANES * (n + 1)] for n, t in enumerate(order[at:at + 2])}, at == 0)
+            send({t: out[:, LANES * n:LANES * (n + 1)] for n, t in enumerate(pair)}, p == 0)
         rest()
         if k == 0 and rounds > 0:
             pl.semaphore_wait(ready.at[rounds - 1], around_me)
@@ -545,6 +584,7 @@
         scratch_shapes=[
             pltpu.VMEM((count, 7 * count), BF16),
             pltpu.VMEM((4 * count, 6 * count), BF16),
+            pltpu.VMEM((2 * count, 6 * count), BF16),
             pltpu.VMEM((3 * LANES, 2 * LANES), BF16),
             pltpu.VMEM((3 * LANES, 2 * LANES), BF16),
             pltpu.VMEM((SUB, area), F32),
@@ -573,6 +613,7 @@
             pltpu.VMEM((count, area), F32),
             pltpu.VMEM(stencils.shape[:1] + stencils.shape[4:], F32),
             pltpu.SemaphoreType.DMA((2,)),
+            pltpu.VMEM((nt // 2, 4, 2 * SUB, 2 * LANES), BF16),
         ],
         compiler_params=pltpu.CompilerParams(collective_id=0, has_side_effects=True, vmem_limit_bytes=48 * 1024 * 1024),
     )

time: 36.5 us -> 36.2 us (level)
  no operation moved by 1% of the time
where the time goes in v5:
time: 36.2 us; the launch traced here: 36 us
  Pallas kernels  35.4 us (98%)
  between operations  0.64 us (2%)
    pallas_call x1, Pallas kernels, shards(): call(*(pltpu.with_memory_space_constraint(x, pltpu.HBM) for x in (start[0...  34.5 us
    pallas_call x1, Pallas kernels, shards(): put(*call(*(pltpu.with_memory_space_constraint(x, pltpu.HBM) for x in (st...  0.88 us

profile of v5, /device:TPU:0, one launch (start us, length us, event | category | flops | bytes accessed | tf_op | source)
XLA Modules:
  0.0 36.0 jit_solution(2615541733696605978)
XLA Ops:
  0.6 34.5 %shard_map.41 = (f32[5,32,1024]{2,1,0:T(8,128)S(1)}, f32[1,2,5]{2,1,0:T(2,128)S(1)}) custom-call(f32[32,1024]{1,0:T(8,128)} %bitcast.3, f32[6,32,32]{2,1,0:T(8,128)} %bitcast.4), custom_call_target="tpu_custom_call" | custom-call | tf_op jit(solution)/shard_map/pallas_call | solution.py:629
  35.2 0.9 %shard_map.42 = (f32[5,32,1024]{2,1,0:T(8,128)}, f32[1,2,5]{2,1,0:T(2,128)}) custom-call(f32[5,32,1024]{2,1,0:T(8,128)S(1)} %get-tuple-element.6.basis, f32[1,2,5]{2,1,0:T(2,128)S(1)} %get-tuple-element.7.coef), custom_call_target="tpu_custom_call" | custom-call | tf_op jit(solution)/shard_map/pallas_call | solution.py:629

commit v6 on v5

--- a/solution.py
+++ b/solution.py
@@ -133,7 +133,7 @@
 
 
 def kernel(sizes, start_in, st_in, basis, coef, mx, my, ym, mz, mzt, ya, yb, wt, field,
-           zs, zr, xs, xz, xr, ys, yz, yr, es, ez, er, edge_slots, rows, hsend, hrecv, rsend, rrecv, ready, ws, start, st, loads, mid):
+           zs, zr, xs, xz, xr, ys, yz, yr, es, ez, er, edge_slots, rows, hsend, hrecv, rsend, rrecv, ready, ws, start, st, loads, mid, us):
     nx, ny, nz = sizes
     total = nx * ny * nz
     count, area = start.shape
@@ -403,17 +403,21 @@
             ws[k, row:row + 1, tile(nt - 1)] += pltpu.roll(edges[2 * d + 1:2 * d + 2], LANES - count, 1)
 
     def send_dots(phase, products):
-        packed = None
-        for k, product in enumerate(products):
-            acc = None
-            for i in range(ni):
-                for t in range(nt):
-                    block = product[SUB * i:SUB * (i + 1), tile(t)]
-                    acc = block if acc is None else acc + block
-            line = jnp.where(iota((SUB, LANES), 0) == k, jnp.sum(acc, axis=0, keepdims=True), 0.0)
-            packed = line if packed is None else packed + line
-        sums = jnp.sum(packed, axis=1, keepdims=True)
-        rows[phase, me] = jnp.sum(jnp.where(diag, sums, 0.0), axis=0, keepdims=True)
+        line = None
+        for base in range(0, len(products), SUB):
+            packed = None
+            for k, product in enumerate(products[base:base + SUB]):
+                acc = None
+                for i in range(ni):
+                    for t in range(nt):
+                        block = product[SUB * i:SUB * (i + 1), tile(t)]
+                        acc = block if acc is None else acc + block
+                part = jnp.where(iota((SUB, LANES), 0) == k, jnp.sum(acc, axis=0, keepdims=True), 0.0)
+                packed = part if packed is None else packed + part
+            sums = jnp.sum(packed, axis=1, keepdims=True)
+            part = jnp.sum(jnp.where(lane8 == iota((SUB, LANES), 0) + base, sums, 0.0), axis=0, keepdims=True)
+            line = part if line is None else line + part
+        rows[phase, me] = line
 
         def send(target):
             pltpu.make_async_remote_copy(
@@ -422,11 +426,15 @@
 
         every_peer(send)
 
-    def take_dots(phase):
+    def take_dots(phase, amount):
         others = rows.at[phase, pl.ds(0, total - 1)]
         pltpu.make_async_copy(others, others, rrecv.at[phase]).wait()
         line = jnp.sum(rows[phase], axis=0)
-        return jnp.sum(jnp.where(diag, line, 0.0), axis=1, keepdims=True)
+        out = []
+        for base in range(0, amount, SUB):
+            sums = jnp.sum(jnp.where(lane8 == iota((SUB, LANES), 0) + base, line, 0.0), axis=1, keepdims=True)
+            out += [sums[i:i + 1] for i in range(min(SUB, amount - base))]
+        return out
 
     pl.semaphore_wait(barrier, around_me)
     send, rest = send_halo(0)
@@ -439,14 +447,23 @@
         call(r)
         if r < rounds - 1:
             pl.semaphore_wait(ready.at[r], around_me)
-    gram, rho = {}, [None]
+    gram, rho = {}, []
+
+    def row_of(k):
+        weighted = wt[...] * us[k]
+        return [weighted * us[i] for i in range(k + 1)]
+
+    def keep(k, sums):
+        for i in range(k + 1):
+            gram[i, k] = sums[i]
 
     def gather(k):
-        sums = take_dots(k)
-        for i in range(k + 1):
-            gram[i, k] = sums[i:i + 1]
-        if k < ITERS:
-            rho.append(sums[k + 1:k + 2] / sums[k:k + 1])
+        lead = 2 if k < ITERS - 1 else 0
+        sums = take_dots(k, lead + k)
+        if lead:
+            rho.append(sums[1] / sums[0])
+        if k > 0:
+            keep(k - 1, sums[lead:])
 
     factor = None
 
@@ -494,18 +511,21 @@
             pl.semaphore_wait(ready.at[rounds - 1], around_me)
         add_edges(k, edges)
         vector = ws[k]
-        weighted = wt[...] * vector
-        send_dots(k, [weighted * ws[i] for i in range(k + 1)] + [field[...] * vector])
-        if k > 0:
+        products = [wt[...] * vector * vector, field[...] * vector] if k < ITERS - 1 else []
+        send_dots(k, products + (row_of(k - 1) if k > 0 else []))
+        if k == 0:
+            us[0] = vector
+        else:
             gather(k - 1)
-            factor = 1.0 / rho[k]
+            factor = 1.0 / rho[k - 1]
+            us[k] = vector * factor - us[k - 1]
     add_yz(ITERS)
     advance(ITERS, True)
     add_x(ITERS)
     advance(ITERS, False)
     add_edges(ITERS, take_edges(ITERS, factor))
-    weighted = wt[...] * ws[ITERS]
-    send_dots(ITERS, [weighted * ws[i] for i in range(ITERS + 1)])
+    us[ITERS] = ws[ITERS] * factor - us[ITERS - 1]
+    send_dots(ITERS, row_of(ITERS - 1) + row_of(ITERS))
     gather(ITERS - 1)
 
     upper, inverse, scale = {}, {}, []
@@ -529,28 +549,30 @@
                 total_i = term if total_i is None else total_i + term
             inverse[i, k] = -total_i * inverse[k, k]
         if k > 0:
-            out = ws[0] * inverse[0, k]
+            out = us[0] * inverse[0, k]
             for i in range(1, k + 1):
-                out = out + ws[i] * inverse[i, k]
+                out = out + us[i] * inverse[i, k]
             basis[k - 1] = out
 
-    for k in range(ITERS):
+    for k in range(ITERS - 1):
         column(k)
     for kind in KINDS:
         sent(kind)
     for phase in range(ITERS):
         others = rows.at[phase, pl.ds(0, total - 1)]
         pltpu.make_async_copy(others, others, rsend.at[phase]).wait()
-    gather(ITERS)
+    sums = take_dots(ITERS, 2 * ITERS + 1)
+    keep(ITERS - 1, sums)
+    keep(ITERS, sums[ITERS:])
+    column(ITERS - 1)
     column(ITERS)
     row2, col2 = iota(coef.shape[1:], 0), iota(coef.shape[1:], 1)
     coefs = jnp.zeros(coef.shape[1:], F32)
     for k in range(ITERS):
-        step = 1.0 if k == 0 else rho[k]
-        alpha = step * (upper[k, k + 1] * inverse[k, k])
+        step = rho[min(k, ITERS - 2)]
+        alpha = step + step * (upper[k, k + 1] * inverse[k, k])
         if k > 0:
-            alpha = alpha + rho[k]
-            alpha = alpha - (1.0 if k == 1 else rho[k - 1]) * (upper[k - 1, k] * inverse[k - 1, k - 1])
+            alpha = alpha - rho[k - 1] * (upper[k - 1, k] * inverse[k - 1, k - 1])
         beta = step * (upper[k + 1, k + 1] * inverse[k, k])
         coefs = jnp.where((row2 == 0) & (col2 == k), alpha, coefs)
         coefs = jnp.where((row2 == 1) & (col2 == k), beta, coefs)
@@ -614,6 +636,7 @@
             pltpu.VMEM(stencils.shape[:1] + stencils.shape[4:], F32),
             pltpu.SemaphoreType.DMA((2,)),
             pltpu.VMEM((nt // 2, 4, 2 * SUB, 2 * LANES), BF16),
+            pltpu.VMEM((halos, count, area), F32),
         ],
         compiler_params=pltpu.CompilerParams(collective_id=0, has_side_effects=True, vmem_limit_bytes=48 * 1024 * 1024),
     )

time: 36.2 us -> 36.3 us (level)
  no operation moved by 1% of the time
where the time goes in v6:
time: 36.3 us; the launch traced here: 36.2 us
  Pallas kernels  35.5 us (98%)
  between operations  0.64 us (2%)
    pallas_call x1, Pallas kernels, shards(): call(*(pltpu.with_memory_space_constraint(x, pltpu.HBM) for x in (start[0...  34.6 us
    pallas_call x1, Pallas kernels, shards(): put(*call(*(pltpu.with_memory_space_constraint(x, pltpu.HBM) for x in (st...  0.88 us

profile of v6, /device:TPU:0, one launch (start us, length us, event | category | flops | bytes accessed | tf_op | source)
XLA Modules:
  0.0 36.2 jit_solution(173957666211958576)
XLA Ops:
  0.6 34.6 %shard_map.41 = (f32[5,32,1024]{2,1,0:T(8,128)S(1)}, f32[1,2,5]{2,1,0:T(2,128)S(1)}) custom-call(f32[32,1024]{1,0:T(8,128)} %bitcast.3, f32[6,32,32]{2,1,0:T(8,128)} %bitcast.4), custom_call_target="tpu_custom_call" | custom-call | tf_op jit(solution)/shard_map/pallas_call | solution.py:652
  35.3 0.9 %shard_map.42 = (f32[5,32,1024]{2,1,0:T(8,128)}, f32[1,2,5]{2,1,0:T(2,128)}) custom-call(f32[5,32,1024]{2,1,0:T(8,128)S(1)} %get-tuple-element.6.basis, f32[1,2,5]{2,1,0:T(2,128)S(1)} %get-tuple-element.7.coef), custom_call_target="tpu_custom_call" | custom-call | tf_op jit(solution)/shard_map/pallas_call | solution.py:652
